TPU v7x, 256 devices: a whole 4x4x8 slice. The times are simulated.
256 devices in a mesh: gx: 8 (over x, core), gy: 8 (over z_lo, y), gz: 4 (over z_hi).
Axes of the slice: x: 4, y: 4, z: 8 (z_hi: 4, z_lo: 2; z = z_hi * 2 + z_lo), core: 2. Of those that a mesh axis runs over, the one named last changes fastest.
Arguments:
- grid_inputs: bfloat16 [186, 512, 1024], P(None, 'gx', 'gy'), may hold values from -6 to 6
- embed_w1: bfloat16 [512, 186], replicated, may hold values from -0.4375 to 0.4375
- embed_b1: float32 [512], replicated, may hold values from -3 to 3
- embed_w2: bfloat16 [512, 512], replicated, may hold values from -0.25 to 0.25
- embed_gain: float32 [512], replicated, may hold values from 0.1 to 1.9
- edge_w1: bfloat16 [512, 1536], replicated, may hold values from -0.15625 to 0.15625
- edge_b1: float32 [512], replicated, may hold values from -3 to 3
- edge_w2: bfloat16 [512, 512], replicated, may hold values from -0.25 to 0.25
- message_gain: float32 [512], replicated, may hold values from 0.1 to 1.9
- message_bias: float32 [512], replicated, may hold values from -3 to 3
- mesh_latent: bfloat16 [512, 8, 8, 256], P('gz', 'gx', 'gy'), may hold values from -6 to 6
- edge_latent: bfloat16 [512, 8, 8, 2048], P('gz', 'gx', 'gy'), may hold values from -6 to 6
- senders: int32 [8, 8, 2048], P('gx', 'gy'), may hold values from 0 to 524287, as said below
- receivers: int32 [8, 8, 2048], P('gx', 'gy'), may hold values from 0 to 16383, as said below
- edge_counts: int32 [8, 8], P('gx', 'gy'), may hold values from 1 to 2048, as said below
Outputs:
- mesh_out: bfloat16 [512, 8, 8, 256], P('gz', 'gx', 'gy')
- grid_latent: bfloat16 [512, 512, 1024], P('gz', 'gx', 'gy')
Inputs may be any that keep to these rules, and one draw needn't show every extreme that they name: `senders`: an edge of tile (b, c) has its sender's row within 8 rows of rows b * 64 to (b + 1) * 64 - 1, clipped to the grid, and its column within 8 columns, cyclically, of columns c * 128 to (c + 1) * 128 - 1; this holds in every slot. `receivers`: an edge of tile t is received by a node of that tile, t * 256 to (t + 1) * 256 - 1, in every slot. `edge_counts`: the live edges of a tile are its first slots; some tile holds 2048 live edges.
All inputs are finite; a program needn't handle non-finite values.
Results may differ from a plain program's by a relative error of at most 0.0049.
Values may be sent and summed in bfloat16 or wider, within the bound.
No kernel may reach another device: no remote copies, remote signals or barrier semaphores. Data moves between devices by JAX's collectives and lax.ppermute only.
A program may use at most 128 MiB of HBM per device.

v0:
```python
import jax
import jax.numpy as jnp
from jax import lax
from jax.sharding import PartitionSpec as P

HALO = 8
BLOCK = 512


epsilon = 1e-05


def padded_2(value, sides, width):
    for axis, dim in sides:
        size, length = (lax.axis_size(axis), value.shape[dim])
        up = [(i, (i + 1) % size) for i in range(size)]
        down = [(j, i) for i, j in up]
        last = lax.slice_in_dim(value, length - width, length, axis=dim)
        first = lax.slice_in_dim(value, 0, width, axis=dim)
        before = lax.ppermute(last, axis, up)
        after = lax.ppermute(first, axis, down)
        value = jnp.concatenate([before, value, after], axis=dim)
    return value


def sent_to_all(value, axis):
    length = lax.axis_size(axis)
    return lax.all_to_all(
        jnp.broadcast_to(value[None], (length, *value.shape)), axis, 0, 0, tiled=True
    )


def joined_along(pieces, dim):
    pieces = jnp.moveaxis(pieces, 0, dim)
    dims = pieces.shape
    return pieces.reshape(*dims[:dim], dims[dim] * dims[dim + 1], *dims[dim + 2 :])


def gather_directly(value, axis, dim):
    pieces = sent_to_all(value, axis)
    return joined_along(pieces, dim)


def cut_along(value, dim, length):
    before, after = (value.shape[:dim], value.shape[dim + 1 :])
    return jnp.moveaxis(value.reshape(*before, length, -1, *after), dim, 0)


def sum_at_owner(value, axis, dim):
    pieces = cut_along(value, dim, lax.axis_size(axis))
    arrived = lax.all_to_all(pieces, axis, split_axis=0, concat_axis=0, tiled=True)
    return arrived.sum(axis=0)


def normalize(values):
    average = jnp.mean(values, axis=0, keepdims=True)
    centred = values - average
    spread = jnp.mean(centred * centred, axis=0, keepdims=True)
    return centred * lax.rsqrt(spread + epsilon)


def embed_cells(flat_inputs, embed_w1, embed_b1, embed_w2, embed_gain):
    grid_hidden = jax.nn.silu(
        jnp.dot(embed_w1, flat_inputs, preferred_element_type=jnp.float32) + embed_b1[:, None]
    ).astype(jnp.bfloat16)
    grid_pre = jnp.dot(embed_w2, grid_hidden, preferred_element_type=jnp.float32)
    return (normalize(grid_pre) * embed_gain[:, None]).astype(jnp.bfloat16)


def lookup_onehot(mesh_pick, live_mask, node_count):
    node_ids = jnp.arange(node_count, dtype=jnp.int32)
    return ((mesh_pick[:, None] == node_ids[None, :]) & live_mask[:, None]).astype(jnp.bfloat16)


def first_layer(weight_rows, bias_rows, edge_block, grid_cols, mesh_cols, latent):
    first_pre = jnp.dot(weight_rows[:, :latent], edge_block, preferred_element_type=jnp.float32)
    first_pre = first_pre + jnp.dot(
        weight_rows[:, latent : 2 * latent], grid_cols, preferred_element_type=jnp.float32
    )
    first_pre = first_pre + jnp.dot(
        weight_rows[:, 2 * latent :], mesh_cols, preferred_element_type=jnp.float32
    )
    return jax.nn.silu(first_pre + bias_rows[:, None]).astype(jnp.bfloat16)


def on_device(
    grid_inputs,
    embed_w1,
    embed_b1,
    embed_w2,
    embed_gain,
    edge_w1,
    edge_b1,
    edge_w2,
    message_gain,
    message_bias,
    mesh_latent,
    edge_latent,
    senders,
    receivers,
    edge_counts,
):
    latent = embed_w2.shape[0]
    channel_count = grid_inputs.shape[0]
    shard_rows = mesh_latent.shape[0]
    lat_rows = grid_inputs.shape[1]
    lon_cols = grid_inputs.shape[2]
    cell_count = lat_rows * lon_cols
    node_count = mesh_latent.shape[3]
    slot_count = edge_latent.shape[3]
    layer_size = lax.axis_size("gz")
    layer_index = lax.axis_index("gz")
    band_index = lax.axis_index("gx")
    sector = lax.axis_index("gy")
    lon_total = lon_cols * lax.axis_size("gy")
    live_count = edge_counts[0, 0]
    padded_cells = (lat_rows + 2 * HALO) * (lon_cols + 2 * HALO)
    row_start = layer_index * shard_rows
    own_latent = embed_cells(
        grid_inputs.reshape(channel_count, cell_count), embed_w1, embed_b1, embed_w2, embed_gain
    ).reshape(latent, lat_rows, lon_cols)
    padded = padded_2(own_latent, (("gx", 1), ("gy", 2)), HALO)
    pad_flat = padded.reshape(latent, padded_cells)
    grid_out = lax.dynamic_slice_in_dim(own_latent, row_start, shard_rows, 0)
    send_all = senders[0, 0]
    lat_local = send_all // lon_total - band_index * lat_rows + HALO
    lon_local = (send_all % lon_total - sector * lon_cols + HALO + lon_total) % lon_total
    grid_index = lat_local * (lon_cols + 2 * HALO) + lon_local
    tile_index = band_index * lax.axis_size("gy") + sector
    near_index = receivers[0, 0] - tile_index * node_count
    slot_ids = jnp.arange(slot_count, dtype=jnp.int32)
    live_all = slot_ids < live_count
    node_ids = jnp.arange(node_count, dtype=jnp.int32)
    degree = jnp.sum(
        ((near_index[:, None] == node_ids[None, :]) & live_all[:, None]).astype(jnp.int32), axis=0
    )
    mesh_own = mesh_latent[:, 0, 0, :]
    edge_own = edge_latent[:, 0, 0, :]
    lead_size, tail_size = (1, slot_count // layer_size)
    arranged = edge_own.reshape(shard_rows, lead_size, layer_size, tail_size)
    assigned = lax.all_to_all(arranged, "gz", split_axis=2, concat_axis=0, tiled=True).reshape(
        latent, lead_size * tail_size
    )
    mesh_full = gather_directly(mesh_own, "gz", 0)
    lead_ids = jnp.arange(lead_size, dtype=jnp.int32)[:, None]
    tail_ids = jnp.arange(tail_size, dtype=jnp.int32)[None, :]
    my_slots = ((lead_ids * layer_size + layer_index) * tail_size + tail_ids).reshape(
        lead_size * tail_size
    )
    my_grid = jnp.take(grid_index, my_slots)
    my_near = jnp.take(near_index, my_slots)
    block_starts = my_slots.reshape(-1, BLOCK)[:, 0]
    live_blocks = jnp.sum((block_starts < live_count).astype(jnp.int32))

    def advance_full(block_index, totals):
        live_mask = my_slots < live_count
        onehot = lookup_onehot(my_near, live_mask, node_count)
        grid_cols = jnp.take(pad_flat, my_grid, axis=1)
        mesh_cols = lax.dot_general(
            mesh_full, onehot, (((1,), (1,)), ((), ())), preferred_element_type=jnp.float32
        ).astype(jnp.bfloat16)
        hidden = first_layer(edge_w1, edge_b1, assigned, grid_cols, mesh_cols, latent)
        second = jnp.dot(edge_w2, hidden, preferred_element_type=jnp.float32)
        message = (
            assigned.astype(jnp.float32)
            + normalize(second) * message_gain[:, None]
            + message_bias[:, None]
        ).astype(jnp.bfloat16)
        return totals + jnp.dot(message, onehot, preferred_element_type=jnp.float32)

    partial_totals = lax.fori_loop(
        0, live_blocks, advance_full, jnp.zeros((latent, node_count), jnp.float32)
    )
    totals_own = sum_at_owner(partial_totals, "gz", 0)
    scale = jnp.maximum(degree, 1).astype(jnp.float32)
    result = mesh_own.astype(jnp.float32) + totals_own / scale[None, :]
    return (result.astype(jnp.bfloat16).reshape(shard_rows, 1, 1, node_count), grid_out)


def solution(mesh):
    return jax.shard_map(
        on_device,
        mesh=mesh,
        in_specs=(
            P(None, "gx", "gy"),
            P(),
            P(),
            P(),
            P(),
            P(),
            P(),
            P(),
            P(),
            P(),
            P("gz", "gx", "gy", None),
            P("gz", "gx", "gy", None),
            P("gx", "gy", None),
            P("gx", "gy", None),
            P("gx", "gy"),
        ),
        out_specs=(P("gz", "gx", "gy", None), P("gz", "gx", "gy")),
        check_vma=False,
    )
```

profile of v0, /device:TPU:32, one launch (start us, length us, event | category | flops | bytes accessed | tf_op | source)
XLA Modules:
  0.0 136.0 jit_solution(17378626972182538780)
XLA Ops:
  0.7 2.6 %pad.17 = bf16[192,64,128]{2,1,0:T(8,128)(2,1)S(1)} pad(bf16[186,64,128]{2,1,0:T(8,128)(2,1)} %param.19, bf16[]{:T(256)} %constant.182), padding=0_6x0_0x0_0 | pad | bytes 6193154
  3.3 4.5 %copy.41 = bf16[24,8,64,128]{3,1,2,0:T(8,128)(2,1)} copy(bf16[24,8,64,128]{3,2,1,0:T(8,128)(2,1)S(1)} %bitcast.62) | data formatting | bytes 6291456
  7.8 14.6 %fusion.45 = (f32[8192]{0:T(1024)S(1)}, f32[8192,512]{1,0:T(8,128)}) fusion(bf16[512,512]{1,0:T(8,128)(2,1)S(1)} %copy-done, bf16[512,186]{0,1:T(8,128)(2,1)S(1)} %copy-done.10, bf16[186,8192]{1,0:T(8,128)(2,1)} %bitcast.63, f32[512]{0:T(512)S(1)} %copy-done.11), kind=kOutput, calls=%fused_computation.84 | convolution fusion | flops 5884600320 | bytes 20574208 | tf_op jit(solution)/shard_map/dot_general | solution.py:66
  22.4 8.6 %multiply_reduce_fusion = f32[8192]{0:T(1024)S(1)} fusion(f32[8192,512]{1,0:T(8,128)} %get-tuple-element.407, f32[8192]{0:T(1024)S(1)} %broadcast_multiply_fusion), kind=kLoop, calls=%fused_computation.4 | loop fusion | flops 12574720 | bytes 16842752 | tf_op jit(solution)/shard_map/reduce_sum | solution.py:58
  31.0 2.0 %copy-done.3 = f32[8192,512]{1,0:T(8,128)S(1)} copy-done((f32[8192,512]{1,0:T(8,128)S(1)}, f32[8192,512]{1,0:T(8,128)}, u32[]{:S(2)}) %copy-start.3) | copy-done | bytes 16777240
  33.1 4.5 %multiply_convert_fusion = bf16[8192,512]{1,0:T(8,128)(2,1)S(1)} fusion(f32[8192,512]{1,0:T(8,128)S(1)} %copy-done.3, f32[512]{0:T(512)S(1)} %copy-done.9, f32[8192]{0:T(1024)S(1)} %add_rsqrt_fusion, f32[8192]{0:T(1024)S(1)} %broadcast_multiply_fusion), kind=kLoop, calls=%fused_computation.3 | loop fusion | flops 16777216 | bytes 25233408 | tf_op jit(solution)/shard_map/convert_element_type | solution.py:67
  37.6 3.2 %copy-done.2 = bf16[8192,512]{1,0:T(8,128)(2,1)} copy-done((bf16[8192,512]{1,0:T(8,128)(2,1)}, bf16[8192,512]{1,0:T(8,128)(2,1)S(1)}, u32[]{:S(2)}) %copy-start.2) | copy-done | bytes 8388632
  42.3 3.0 %collective-permute-start.1 = (bf16[512,8,128]{0,2,1:T(8,128)(2,1)}, bf16[512,8,128]{0,2,1:T(8,128)(2,1)S(1)}, u32[]{:S(2)}, u32[]{:S(2)}) collective-permute-start(bf16[512,8,128]{0,2,1:T(8,128)(2,1)} %get-tuple-element.405), channel_id=1, source_target_pairs={{32,0},{64,32},{96,64},{128,96},{160,128},{192,160},{224,192},{0,2... | collective-permute-start | bytes 3145736 | tf_op jit(solution)/shard_map/ppermute | solution.py:21
  46.5 7.6 %all-to-all-start = ((bf16[128,1,4,512]{3,0,1,2:T(8,128)(2,1)}), bf16[128,1,4,512]{3,0,1,2:T(8,128)(2,1)S(1)}, u32[]{:S(2)}, u32[]{:S(2)}) async-start(bf16[128,1,4,512]{3,0,1,2:T(8,128)(2,1)} %copy.34), calls=%async_computation | async-start | bytes 1048576 | tf_op jit(solution)/shard_map/all_to_all | solution.py:141
  54.8 3.1 %gather_fusion.1 = s32[512]{0:T(512)S(1)} fusion(s32[2048]{0:T(1024)S(1)} %fusion.35, s32[1024]{0:T(1024)S(1)} %pad_clamp_fusion.1), kind=kCustom, calls=%fused_computation.clone | custom fusion | bytes 6144 | tf_op jit(solution)/shard_map/jit(_take)/gather | solution.py:150
  58.0 2.4 %pad_maximum_fusion.3 = (bf16[512,80,8]{0,2,1:T(8,128)(2,1)}, bf16[512,80,8]{0,2,1:T(8,128)(2,1)}) fusion(bf16[512,8,128]{0,2,1:T(8,128)(2,1)S(1)} %collective-permute-done.1, bf16[512,64,128]{0,2,1:T(8,128)(2,1)} %bitcast.58, bf16[512,8,128]{0,2,1:T(8,128)(2,1)S(1)} %collective-permute-done), kind=kLoop, calls=%fused_computation.24 | loop fusion | flops 3932160 | bytes 11796480 | tf_op jit(solution)/shard_map/slice | solution.py:18
  62.0 2.6 %collective-permute-start.3 = (bf16[512,80,8]{0,2,1:T(8,128)(2,1)}, bf16[512,80,8]{0,2,1:T(8,128)(2,1)}, u32[]{:S(2)}, u32[]{:S(2)}) collective-permute-start(bf16[512,80,8]{0,2,1:T(8,128)(2,1)} %get-tuple-element.403), channel_id=1, source_target_pairs={{4,0},{8,4},{12,8},{16,12},{20,16},{24,20},{28,24},{0,28},{5,1},{9... | collective-permute-start | bytes 1966088 | tf_op jit(solution)/shard_map/ppermute | solution.py:21
  64.6 3.1 %gather_fusion.2 = s32[512]{0:T(512)S(1)} fusion(s32[2048]{0:T(1024)S(1)} %bitcast.55, s32[1024]{0:T(1024)S(1)} %pad_clamp_fusion.1), kind=kCustom, calls=%fused_computation.1.clone | custom fusion | bytes 6144 | tf_op jit(solution)/shard_map/jit(_take)/gather | solution.py:151
  70.2 5.8 %all-to-all-start.1 = ((bf16[4,128,256]{2,1,0:T(8,128)(2,1)}), bf16[4,128,256]{2,1,0:T(8,128)(2,1)S(1)}, u32[]{:S(2)}, u32[]{:S(2)}) async-start(bf16[4,128,256]{2,1,0:T(8,128)(2,1)} %broadcast_in_dim.53), calls=%async_computation.1 | async-start | bytes 524288 | tf_op jit(solution)/shard_map/all_to_all | solution.py:28
  76.0 2.4 %fusion.16 = f32[512,512]{1,0:T(8,128)} fusion(bf16[512,512]{1,0:T(8,128)(2,1)S(1)} %bitcast.65, bf16[512,1536]{1,0:T(8,128)(2,1)} %param.24), kind=kOutput, calls=%fused_computation.34 | convolution fusion | flops 268435456 | bytes 2097152 | tf_op jit(solution)/shard_map/while/body/dot_general | solution.py:76
  78.4 6.2 %collective-permute-done.2 = bf16[512,80,8]{0,2,1:T(8,128)(2,1)} collective-permute-done((bf16[512,80,8]{0,2,1:T(8,128)(2,1)}, bf16[512,80,8]{0,2,1:T(8,128)(2,1)}, u32[]{:S(2)}, u32[]{:S(2)}) %collective-permute-start.2) | collective-permute-done | bytes 655392 | tf_op jit(solution)/shard_map/ppermute | solution.py:20
  84.6 12.1 %pad_maximum_fusion = bf16[512,80,144]{0,2,1:T(8,128)(2,1)} fusion(bf16[512,80,8]{0,2,1:T(8,128)(2,1)} %collective-permute-done.3, bf16[512,8,128]{0,2,1:T(8,128)(2,1)S(1)} %collective-permute-done.1, bf16[512,64,128]{0,2,1:T(8,128)(2,1)} %bitcast.59, bf16[512,8,128]{0,2,1:T(8,128)(2,1)S(1)} %collective-permute-done, ...), kind=kLoop, calls=%fused_computation.6 | loop fusion | flops 58982400 | bytes 23592960 | tf_op jit(solution)/shard_map/concatenate | solution.py:22
  96.7 7.9 %gather_fusion = bf16[512,512]{1,0:T(8,128)(2,1)S(1)} fusion(bf16[512,11520]{0,1:T(8,128)(2,1)} %bitcast.61, s32[1024]{0:T(1024)S(1)} %pad_clamp_fusion), kind=kCustom, calls=%fused_computation.2 | custom fusion | bytes 1050624 | tf_op jit(solution)/shard_map/while/body/jit(_take)/gather | solution.py:158
  104.7 1.9 %fusion.3 = f32[512,512]{1,0:T(8,128)S(1)} fusion(f32[512,512]{1,0:T(8,128)} %fusion.16, bf16[512,512]{1,0:T(8,128)(2,1)S(1)} %gather_fusion, bf16[512,1536]{1,0:T(8,128)(2,1)} %param.24, pred[512]{0:T(512)(128)(4,1)S(1)} %get-tuple-element.400), kind=kOutput, calls=%fused_computation.14 | convolution fusion | flops 268959744 | bytes 3146240 | tf_op jit(solution)/shard_map/while/body/dot_general | solution.py:77
  106.6 1.9 %multiply_convert_fusion.2 = bf16[512,512]{1,0:T(8,128)(2,1)S(1)} fusion(f32[512,512]{1,0:T(8,128)S(1)} %fusion.3, bf16[512,256]{1,0:T(8,128)(2,1)S(1)} %bitcast.67, f32[512]{0:T(512)S(1)} %copy-done.12, bf16[512,1536]{1,0:T(8,128)(2,1)} %param.24, s32[512]{0:T(512)S(1)} %broadcast_select_fusion, pred[512]{0:T(512)(128)(4,1)S(1)} %fusion.41), kind=kOutput, calls=%fused_computation.20 | convolution fusion | flops 405012480 | bytes 2363904 | tf_op jit(solution)/shard_map/while/body/dot_general | solution.py:80
  110.7 1.9 %while.17 = (s32[]{:T(128)}, f32[512,256]{1,0:T(8,128)}, s32[]{:T(128)}, f32[512,256]{1,0:T(8,128)S(1)}, s32[]{:T(128)}) while((s32[]{:T(128)}, f32[512,256]{1,0:T(8,128)}, s32[]{:T(128)}, f32[512,256]{1,0:T(8,128)S(1)}, s32[]{:T(128)}) %tuple.53), condition=%wide.region_5.7_spmd, body=%wide.region_4.6_spmd.sunk | while | flops 131074 | bytes 1572925 | solution.py:171
  112.6 5.8 %all-to-all-start.2 = ((f32[4,128,256]{2,1,0:T(8,128)}), f32[4,128,256]{2,1,0:T(8,128)S(1)}, u32[]{:S(2)}, u32[]{:S(2)}) async-start(f32[4,128,256]{2,1,0:T(8,128)} %bitcast.19), calls=%async_computation.2 | async-start | bytes 1048576 | tf_op jit(solution)/shard_map/all_to_all | solution.py:51
  120.1 2.8 %copy.40 = bf16[128,64,128]{2,1,0:T(8,128)(2,1)} copy(bf16[128,64,128]{0,2,1:T(8,128)(2,1)S(1)} %constant_dynamic-slice_fusion) | data formatting | bytes 4194304
  124.2 11.0 %all-to-all-done.2 = f32[4,128,256]{2,1,0:T(8,128)S(1)} async-done(((f32[4,128,256]{2,1,0:T(8,128)}), f32[4,128,256]{2,1,0:T(8,128)S(1)}, u32[]{:S(2)}, u32[]{:S(2)}) %all-to-all-start.2) | async-done | bytes 524320 | tf_op jit(solution)/shard_map/all_to_all | solution.py:51
  (63 shorter events, 14.7 us)
Async XLA Ops:
  0.6 7.2 %copy-start = (bf16[512,512]{1,0:T(8,128)(2,1)S(1)}, bf16[512,512]{1,0:T(8,128)(2,1)}, u32[]{:S(2)}) copy-start(bf16[512,512]{1,0:T(8,128)(2,1)} %param.22) | copy-start | bytes 1572868
  0.6 7.1 %copy-start.10 = (bf16[512,186]{0,1:T(8,128)(2,1)S(1)}, bf16[512,186]{0,1:T(8,128)(2,1)}, u32[]{:S(2)}) copy-start(bf16[512,186]{0,1:T(8,128)(2,1)} %param.20) | copy-start | bytes 571396
  0.7 7.1 %copy-start.11 = (f32[512]{0:T(512)S(1)}, f32[512]{0:T(512)}, u32[]{:S(2)}) copy-start(f32[512]{0:T(512)} %param.21) | copy-start | bytes 6148
  22.4 10.7 %copy-start.3 = (f32[8192,512]{1,0:T(8,128)S(1)}, f32[8192,512]{1,0:T(8,128)}, u32[]{:S(2)}) copy-start(f32[8192,512]{1,0:T(8,128)} %get-tuple-element.407) | copy-start | bytes 50331652
  22.4 10.7 %copy-start.9 = (f32[512]{0:T(512)S(1)}, f32[512]{0:T(512)}, u32[]{:S(2)}) copy-start(f32[512]{0:T(512)} %param.23) | copy-start | bytes 6148
  33.0 12.2 %copy-start.5 = (bf16[128,1,1,2048]{3,0,2,1:T(8,128)(2,1)S(1)}, bf16[128,1,1,2048]{3,0,2,1:T(8,128)(2,1)}, u32[]{:S(2)}) copy-start(bf16[128,1,1,2048]{3,0,2,1:T(8,128)(2,1)} %param.30) | copy-start | bytes 1572868
  33.0 21.7 %copy-start.7 = (s32[1,1,2048]{2,1,0:T(1,128)S(1)}, s32[1,1,2048]{2,1,0:T(1,128)}, u32[]{:S(2)}) copy-start(s32[1,1,2048]{2,1,0:T(1,128)} %param.31) | copy-start | bytes 24580
  33.0 24.9 %copy-start.8 = (s32[1,1,2048]{2,1,0:T(1,128)S(1)}, s32[1,1,2048]{2,1,0:T(1,128)}, u32[]{:S(2)}) copy-start(s32[1,1,2048]{2,1,0:T(1,128)} %param.32) | copy-start | bytes 24580
  37.5 3.2 %copy-start.2 = (bf16[8192,512]{1,0:T(8,128)(2,1)}, bf16[8192,512]{1,0:T(8,128)(2,1)S(1)}, u32[]{:S(2)}) copy-start(bf16[8192,512]{1,0:T(8,128)(2,1)S(1)} %multiply_convert_fusion) | copy-start | bytes 25165828
  37.6 31.9 %copy-start.6 = (bf16[128,1,1,256]{3,0,2,1:T(8,128)(2,1)S(1)}, bf16[128,1,1,256]{3,0,2,1:T(8,128)(2,1)}, u32[]{:S(2)}) copy-start(bf16[128,1,1,256]{3,0,2,1:T(8,128)(2,1)} %param.29) | copy-start | bytes 196612
  42.3 15.7 %collective-permute-start = (bf16[512,8,128]{0,2,1:T(8,128)(2,1)}, bf16[512,8,128]{0,2,1:T(8,128)(2,1)S(1)}, u32[]{:S(2)}, u32[]{:S(2)}) collective-permute-start(bf16[512,8,128]{0,2,1:T(8,128)(2,1)} %get-tuple-element.404), channel_id=1, source_target_pairs={{0,32},{32,64},{64,96},{96,128},{128,160},{160,192},{192,224},{224... | collective-permute-start | bytes 3145736 | tf_op jit(solution)/shard_map/ppermute | solution.py:20
  42.3 15.7 %collective-permute-start.1 = (bf16[512,8,128]{0,2,1:T(8,128)(2,1)}, bf16[512,8,128]{0,2,1:T(8,128)(2,1)S(1)}, u32[]{:S(2)}, u32[]{:S(2)}) collective-permute-start(bf16[512,8,128]{0,2,1:T(8,128)(2,1)} %get-tuple-element.405), channel_id=1, source_target_pairs={{32,0},{64,32},{96,64},{128,96},{160,128},{192,160},{224,192},{0,2... | collective-permute-start | bytes 3145736 | tf_op jit(solution)/shard_map/ppermute | solution.py:21
  46.5 22.9 %all-to-all-start = ((bf16[128,1,4,512]{3,0,1,2:T(8,128)(2,1)}), bf16[128,1,4,512]{3,0,1,2:T(8,128)(2,1)S(1)}, u32[]{:S(2)}, u32[]{:S(2)}) async-start(bf16[128,1,4,512]{3,0,1,2:T(8,128)(2,1)} %copy.34), calls=%async_computation | async-start | bytes 1048576 | tf_op jit(solution)/shard_map/all_to_all | solution.py:141
  60.4 24.2 %collective-permute-start.2 = (bf16[512,80,8]{0,2,1:T(8,128)(2,1)}, bf16[512,80,8]{0,2,1:T(8,128)(2,1)}, u32[]{:S(2)}, u32[]{:S(2)}) collective-permute-start(bf16[512,80,8]{0,2,1:T(8,128)(2,1)} %get-tuple-element.402), channel_id=1, source_target_pairs={{0,4},{4,8},{8,12},{12,16},{16,20},{20,24},{24,28},{28,0},{1,5},{5... | collective-permute-start | bytes 1966088 | tf_op jit(solution)/shard_map/ppermute | solution.py:20
  62.0 22.6 %collective-permute-start.3 = (bf16[512,80,8]{0,2,1:T(8,128)(2,1)}, bf16[512,80,8]{0,2,1:T(8,128)(2,1)}, u32[]{:S(2)}, u32[]{:S(2)}) collective-permute-start(bf16[512,80,8]{0,2,1:T(8,128)(2,1)} %get-tuple-element.403), channel_id=1, source_target_pairs={{4,0},{8,4},{12,8},{16,12},{20,16},{24,20},{28,24},{0,28},{5,1},{9... | collective-permute-start | bytes 1966088 | tf_op jit(solution)/shard_map/ppermute | solution.py:21
  70.2 36.5 %all-to-all-start.1 = ((bf16[4,128,256]{2,1,0:T(8,128)(2,1)}), bf16[4,128,256]{2,1,0:T(8,128)(2,1)S(1)}, u32[]{:S(2)}, u32[]{:S(2)}) async-start(bf16[4,128,256]{2,1,0:T(8,128)(2,1)} %broadcast_in_dim.53), calls=%async_computation.1 | async-start | bytes 524288 | tf_op jit(solution)/shard_map/all_to_all | solution.py:28
  78.4 28.2 %copy-start.12 = (f32[512]{0:T(512)S(1)}, f32[512]{0:T(512)}, u32[]{:S(2)}) copy-start(f32[512]{0:T(512)} %param.25) | copy-start | bytes 6148
  96.7 11.9 %copy-start.4 = (bf16[512,512]{1,0:T(8,128)(2,1)S(1)}, bf16[512,512]{1,0:T(8,128)(2,1)}, u32[]{:S(2)}) copy-start(bf16[512,512]{1,0:T(8,128)(2,1)} %param.26) | copy-start | bytes 1572868
  96.7 12.5 %copy-start.13 = (f32[512]{0:T(512)S(1)}, f32[512]{0:T(512)}, u32[]{:S(2)}) copy-start(f32[512]{0:T(512)} %param.28) | copy-start | bytes 6148
  96.7 12.5 %copy-start.14 = (f32[512]{0:T(512)S(1)}, f32[512]{0:T(512)}, u32[]{:S(2)}) copy-start(f32[512]{0:T(512)} %param.27) | copy-start | bytes 6148
  106.6 29.3 %copy-start.1 = (bf16[512,512]{1,0:T(8,128)(2,1)S(1)}, bf16[512,512]{1,0:T(8,128)(2,1)}, u32[]{:S(2)}) copy-start(bf16[512,512]{1,0:T(8,128)(2,1)} %param.22) | copy-start | bytes 1572868
  112.6 22.7 %all-to-all-start.2 = ((f32[4,128,256]{2,1,0:T(8,128)}), f32[4,128,256]{2,1,0:T(8,128)S(1)}, u32[]{:S(2)}, u32[]{:S(2)}) async-start(f32[4,128,256]{2,1,0:T(8,128)} %bitcast.19), calls=%async_computation.2 | async-start | bytes 1048576 | tf_op jit(solution)/shard_map/all_to_all | solution.py:51
where the time goes:
time: 137 us; the launch traced here: 136 us
  local copies, waits for them, and re-layouts  35.5 us (26%)
  other arithmetic  31.9 us (23%)
  starting transfers between devices  26.2 us (19%)
  matrix products  21.9 us (16%)
  waiting for transfers between devices  18.9 us (14%)
  between operations  1.59 us (1%)
    unnamed x34, local copies, waits for them, and re-layouts  15.5 us
    dot_general x1, matrix products, embed_cells(): jnp.dot(embed_w2, grid_hidden, preferred_element_type=jnp.float32)  14.6 us
    concatenate x1, other arithmetic, padded_2(): value = jnp.concatenate([before, value, after], axis=dim)  12.1 us
    all_to_all x1, waiting for transfers between devices, sum_at_owner(): lax.all_to_all(pieces, axis, split_axis=0, concat_axis=0, tiled=True)  11 us
    reduce_sum x2, other arithmetic, normalize(): spread = jnp.mean(centred * centred, axis=0, keepdims=True)  8.8 us
    gather x1, local copies, waits for them, and re-layouts, advance_full(): grid_cols = jnp.take(pad_flat, my_grid, axis=1)  7.91 us
    all_to_all x1, starting transfers between devices, on_device(): lax.all_to_all(arranged, 'gz', split_axis=2, concat_axis=0, tiled=True)  7.56 us
    ppermute x2, waiting for transfers between devices, padded_2(): before = lax.ppermute(last, axis, up)  6.18 us
  transfers between devices with their start and end apart: 7, of which 3 were waited for; matrix products, arithmetic and copies ran while one was open for 30% of the time, Pallas kernels for 0%

commit v1 on v0

v1 whole, which is shorter than its diff:
```python
import functools

import jax
import jax.numpy as jnp
from jax import lax
from jax.experimental import pallas as pl
from jax.experimental.pallas import tpu as pltpu
from jax.sharding import PartitionSpec as P

HALO = 8
LANES = 128
DEPTH = 192
ONES = 3

epsilon = 1e-05


def normalized(values):
    scale = 1.0 / values.shape[0]
    average = jnp.sum(values, axis=0, keepdims=True) * scale
    centred = values - average
    spread = jnp.sum(centred * centred, axis=0, keepdims=True) * scale
    return average, lax.rsqrt(spread + epsilon)


def silu_of_half(half):
    return (half + half * jnp.tanh(half)).astype(jnp.bfloat16)


def dot(a, b):
    return jnp.dot(a, b, preferred_element_type=jnp.float32)


def call(body, name, grid=None, **kw):
    return pl.pallas_call(body, name=name, **kw)


def planes_kernel(x_ref, out_ref, left_ref, right_ref, wide_ref, left_acc, right_acc):
    channels, rows, lanes = x_ref.shape
    step = pl.program_id(0)
    wide_ref[...] = x_ref[...].astype(jnp.float32).reshape(channels * rows, lanes)
    extra = DEPTH - channels
    tail_ids = lax.broadcasted_iota(jnp.int32, (extra, lanes), 0)
    tail = jnp.where(tail_ids < ONES, 1.0, 0.0)
    lane_ids = lax.broadcasted_iota(jnp.int32, (DEPTH, lanes), 1)
    group = lanes // HALO
    half = step % (group // rows)
    left = left_acc[...]
    right = right_acc[...]
    for r in range(rows):
        plane = wide_ref[pl.ds(r, channels, stride=rows), :]
        plane = jnp.concatenate([plane, tail], axis=0)
        out_ref[:, r * lanes : (r + 1) * lanes] = plane.astype(jnp.bfloat16)
        first = (half * rows + r) * HALO
        mine = (lane_ids >= first) & (lane_ids < first + HALO)
        left = jnp.where(mine, pltpu.roll(plane, first, 1), left)
        right = jnp.where(mine, pltpu.roll(plane, first + HALO, 1), right)
    left_acc[...] = left
    right_acc[...] = right
    left_ref[...] = left.astype(jnp.bfloat16)
    right_ref[...] = right.astype(jnp.bfloat16)


def planes_of(grid_inputs):
    channels, rows, lanes = grid_inputs.shape
    block = 8
    per_plane = lanes // HALO // block
    packed = jax.ShapeDtypeStruct((DEPTH, rows * HALO), jnp.bfloat16)
    return pl.pallas_call(
        planes_kernel,
        name="planes",
        grid=(rows // block,),
        in_specs=[pl.BlockSpec((channels, block, lanes), lambda i: (0, i, 0))],
        out_specs=[
            pl.BlockSpec((DEPTH, block * lanes), lambda i: (0, i)),
            pl.BlockSpec((DEPTH, lanes), lambda i: (0, i // per_plane)),
            pl.BlockSpec((DEPTH, lanes), lambda i: (0, i // per_plane)),
        ],
        out_shape=[jax.ShapeDtypeStruct((DEPTH, rows * lanes), jnp.bfloat16), packed, packed],
        scratch_shapes=[
            pltpu.VMEM((channels * block, lanes), jnp.float32),
            pltpu.VMEM((DEPTH, lanes), jnp.float32),
            pltpu.VMEM((DEPTH, lanes), jnp.float32),
        ],
    )(grid_inputs)


def corners_kernel(up_ref, down_ref, left_in, right_in, left_ref, right_ref):
    lanes = LANES
    own = left_in.shape[1]
    left_ref[:, :own] = left_in[...]
    right_ref[:, :own] = right_in[...]
    lane_ids = lax.broadcasted_iota(jnp.int32, (DEPTH, lanes), 1)
    left = jnp.zeros((DEPTH, lanes), jnp.float32)
    right = jnp.zeros((DEPTH, lanes), jnp.float32)
    for r in range(2 * HALO):
        source = up_ref if r < HALO else down_ref
        at = (r % HALO) * lanes
        plane = source[:, at : at + lanes].astype(jnp.float32)
        first = r * HALO
        mine = (lane_ids >= first) & (lane_ids < first + HALO)
        left = jnp.where(mine, pltpu.roll(plane, first, 1) if first else plane, left)
        right = jnp.where(mine, pltpu.roll(plane, (first + HALO) % lanes, 1) if (first + HALO) % lanes else plane, right)
    left_ref[:, own:] = left.astype(jnp.bfloat16)
    right_ref[:, own:] = right.astype(jnp.bfloat16)


def with_corners(up, down, left, right):
    packed = jax.ShapeDtypeStruct((DEPTH, left.shape[1] + LANES), jnp.bfloat16)
    return pl.pallas_call(corners_kernel, name="corners", out_shape=[packed, packed])(up, down, left, right)


def embed_kernel(layer_ref, x_ref, w1_ref, wa, wb, wc, wd, gain_ref, *rest, chunk):
    out_ref, acc_ref, wide_ref = rest[-3:]
    keep, rows, lanes = out_ref.shape
    w1 = w1_ref[...]
    gain = gain_ref[...]
    for at in range(0, rows * lanes, chunk):
        hidden = silu_of_half(dot(w1, x_ref[:, at : at + chunk]))
        w2 = jnp.concatenate([wa[...], wb[...], wc[...], wd[...]], axis=0)
        values = dot(w2, hidden)
        average, factor = normalized(values)
        latent = (values[:keep] - average) * factor * gain
        for r in range(chunk // lanes):
            wide_ref[pl.ds(at // lanes + r, keep, stride=rows), :] = latent[:, r * lanes : (r + 1) * lanes]
    out_ref[...] = wide_ref[...].reshape(keep, rows, lanes).astype(jnp.bfloat16)


def embed_rows(layer, planes, w1, w2, gain, rows_total, first, count, earlier=None, block=8, chunk=512):
    latent = w2.shape[0]
    keep = latent // 4
    lanes = LANES
    begin = first // block
    turn = lambda k: (lambda i, s: ((s[0] + k) % 4, 0))
    args = [layer, planes, w1, w2, w2, w2, w2, gain]
    in_specs = [
        pl.BlockSpec((DEPTH, block * lanes), lambda i, s: (0, i + begin)),
        pl.BlockSpec(w1.shape, lambda i, s: (0, 0)),
        pl.BlockSpec((keep, latent), turn(0)),
        pl.BlockSpec((keep, latent), turn(1)),
        pl.BlockSpec((keep, latent), turn(2)),
        pl.BlockSpec((keep, latent), turn(3)),
        pl.BlockSpec((keep, 1), turn(0)),
    ]
    aliases = {}
    if earlier is not None:
        args.append(earlier)
        in_specs.append(pl.BlockSpec(memory_space=pl.ANY))
        aliases = {8: 0}
    cells = count * lanes
    return pl.pallas_call(
        functools.partial(embed_kernel, chunk=chunk),
        name="embed",
        grid_spec=pltpu.PrefetchScalarGridSpec(
            num_scalar_prefetch=1,
            grid=(count // block,),
            in_specs=in_specs,
            out_specs=pl.BlockSpec((keep, block, lanes), lambda i, s: (0, i + begin, 0)),
            scratch_shapes=[
                pltpu.VMEM((8, 128), jnp.float32),
                pltpu.VMEM((keep * block, lanes), jnp.float32),
            ],
        ),
        out_shape=jax.ShapeDtypeStruct((keep, rows_total, lanes), jnp.bfloat16),
        input_output_aliases=aliases,
        cost_estimate=pl.CostEstimate(
            flops=2 * cells * latent * (256 + latent), transcendentals=cells * latent, bytes_accessed=cells * 640
        ),
    )(*args)


def sender_kernel(pick_ref, x_ref, up_ref, down_ref, left_ref, right_ref, w1_ref, w2_ref, gain_ref, out_ref):
    slots = pick_ref.shape[1]
    pick = pick_ref[...]

    def picked(ref, begin, at, width):
        ids = lax.broadcasted_iota(jnp.int32, (width, slots), 0) + (begin + at)
        chosen = jnp.where(ids == pick, 1.0, 0.0).astype(jnp.bfloat16)
        return dot(ref[:, at : at + width], chosen)

    total = jnp.zeros((DEPTH, slots), jnp.float32)
    begin = 0
    for ref in (x_ref, up_ref, down_ref, left_ref, right_ref):
        size = ref.shape[1]
        width = min(size, 1024)
        for at in range(0, size, width):
            total = total + picked(ref, begin, at, width)
        begin += size
    hidden = silu_of_half(dot(w1_ref[...], total.astype(jnp.bfloat16)))
    values = dot(w2_ref[...], hidden)
    average, factor = normalized(values)
    out_ref[...] = ((values - average) * factor * gain_ref[...]).astype(jnp.bfloat16)


def sender_latents(pick, planes, up, down, left, right, w1, w2, gain):
    slots = pick.shape[1]
    latent = w2.shape[0]
    cells = planes.shape[1] + 2 * up.shape[1] + 2 * left.shape[1]
    return pl.pallas_call(
        sender_kernel,
        name="senders",
        out_shape=jax.ShapeDtypeStruct((latent, slots), jnp.bfloat16),
        cost_estimate=pl.CostEstimate(flops=2 * cells * 256 * slots, transcendentals=0, bytes_accessed=cells * 400),
    )(pick, planes, up, down, left, right, w1, w2, gain)


def edge_kernel(live_ref, near_ref, all_near_ref, in_ref, send_ref, w1_ref, b1_ref, w2_ref, gain_ref, bias_ref, out_ref, degree_ref):
    latent = w2_ref.shape[0]
    slots = near_ref.shape[1]
    nodes = out_ref.shape[1]
    edge = in_ref[:, :slots]
    mesh = in_ref[:, slots:]
    near = near_ref[...]
    node_ids = lax.broadcasted_iota(jnp.int32, (nodes, slots), 0)
    onehot = jnp.where(node_ids == near, 1.0, 0.0).astype(jnp.bfloat16)
    mesh_cols = dot(mesh, onehot).astype(jnp.bfloat16)
    first = dot(w1_ref[:, :latent], edge) + dot(w1_ref[:, latent : 2 * latent], send_ref[...])
    first = first + dot(w1_ref[:, 2 * latent :], mesh_cols) + b1_ref[...]
    hidden = silu_of_half(0.5 * first)
    second = dot(w2_ref[...], hidden)
    average, factor = normalized(second)
    message = edge.astype(jnp.float32) + (second - average) * factor * gain_ref[...] + bias_ref[...]
    slot_ids = lax.broadcasted_iota(jnp.int32, (nodes, slots), 1) + live_ref[1]
    counted = jnp.where((node_ids == near) & (slot_ids < live_ref[0]), 1.0, 0.0).astype(jnp.bfloat16)
    nt = (((1,), (1,)), ((), ()))
    out_ref[...] = lax.dot_general(
        message.astype(jnp.bfloat16), counted, nt, preferred_element_type=jnp.float32
    ).astype(jnp.bfloat16)
    every = all_near_ref.shape[1]
    node_all = lax.broadcasted_iota(jnp.int32, (nodes, every), 0)
    slot_all = lax.broadcasted_iota(jnp.int32, (nodes, every), 1)
    counted_all = jnp.where((node_all == all_near_ref[...]) & (slot_all < live_ref[0]), 1.0, 0.0).astype(jnp.bfloat16)
    degree_ref[...] = lax.dot_general(
        jnp.ones((8, every), jnp.bfloat16), counted_all, nt, preferred_element_type=jnp.float32
    )


def edge_sums(live, near, all_near, arrived, send, w1, b1, w2, gain, bias, nodes):
    latent = w2.shape[0]
    vmem = pl.BlockSpec(memory_space=pltpu.VMEM)
    return pl.pallas_call(
        edge_kernel,
        name="edges",
        in_specs=[pl.BlockSpec(memory_space=pltpu.SMEM)] + [vmem] * 9,
        out_shape=[
            jax.ShapeDtypeStruct((latent, nodes), jnp.bfloat16),
            jax.ShapeDtypeStruct((8, nodes), jnp.float32),
        ],
        cost_estimate=pl.CostEstimate(
            flops=2 * near.shape[1] * latent * (5 * latent), transcendentals=0, bytes_accessed=1 << 22
        ),
    )(live, near, all_near, arrived, send, w1, b1, w2, gain, bias)


def with_bias_columns(weight, bias):
    parts = []
    left = bias
    for _ in range(ONES):
        part = lax.reduce_precision(left, 8, 7)
        parts.append(part)
        left = left - part
    rest = DEPTH - weight.shape[1] - ONES
    columns = jnp.stack(parts + [jnp.zeros_like(bias)] * rest, axis=1)
    return jnp.concatenate([weight, columns.astype(jnp.bfloat16)], axis=1) * jnp.bfloat16(0.5)


def shifted(value, axis, by):
    size = lax.axis_size(axis)
    return lax.ppermute(value, axis, [(i, (i + by) % size) for i in range(size)])


def on_device(
    grid_inputs,
    embed_w1,
    embed_b1,
    embed_w2,
    embed_gain,
    edge_w1,
    edge_b1,
    edge_w2,
    message_gain,
    message_bias,
    mesh_latent,
    edge_latent,
    senders,
    receivers,
    edge_counts,
):
    latent = embed_w2.shape[0]
    shard_rows = mesh_latent.shape[0]
    lat_rows, lon_cols = grid_inputs.shape[1:]
    node_count = mesh_latent.shape[3]
    slot_count = edge_latent.shape[3]
    layers = lax.axis_size("gz")
    share = slot_count // layers
    layer = lax.axis_index("gz")
    band = lax.axis_index("gx")
    sector = lax.axis_index("gy")
    lon_total = lon_cols * lax.axis_size("gy")
    live_count = edge_counts[0, 0]
    mesh_own = mesh_latent[:, 0, 0, :]
    edge_own = edge_latent[:, 0, 0, :]

    shares = edge_own.reshape(shard_rows, layers, share).transpose(1, 0, 2)
    outgoing = jnp.concatenate(
        [shares, jnp.broadcast_to(mesh_own[None], (layers, shard_rows, node_count))], axis=2
    )
    arrived = lax.all_to_all(outgoing, "gz", 0, 0, tiled=True).reshape(latent, share + node_count)

    planes, left, right = planes_of(grid_inputs)
    width = HALO * lon_cols
    from_up = shifted(planes[:, -width:], "gx", 1)
    from_down = shifted(planes[:, :width], "gx", -1)
    left, right = with_corners(from_up, from_down, left, right)
    from_left = shifted(right, "gy", 1)
    from_right = shifted(left, "gy", -1)

    mine = lambda a: lax.dynamic_slice_in_dim(a, layer * share, share, 0)[None]
    send_all = mine(senders[0, 0])
    lat = send_all // lon_total - band * lat_rows
    lon = (send_all % lon_total - sector * lon_cols + HALO + lon_total) % lon_total - HALO
    inside_lon = (lon >= 0) & (lon < lon_cols)
    own = lat_rows * lon_cols
    side = (lat_rows + 2 * HALO) * HALO
    at_row = jnp.where(
        lat < 0, own + (lat + HALO) * lon_cols, jnp.where(lat < lat_rows, lat * lon_cols, own + width + (lat - lat_rows) * lon_cols)
    )
    at_side = jnp.where(
        lat < 0, (lat_rows + lat + HALO) * HALO, jnp.where(lat < lat_rows, lat * HALO, (lat + HALO) * HALO)
    )
    at_side = at_side + own + 2 * width
    pick = jnp.where(
        inside_lon, at_row + lon, jnp.where(lon < 0, at_side + lon + HALO, at_side + side + lon - lon_cols)
    )
    tile = band * lax.axis_size("gy") + sector
    near_all = receivers[0] - tile * node_count
    near = mine(near_all[0])

    w1 = with_bias_columns(embed_w1, embed_b1)
    gain = embed_gain[:, None]
    layer_arg = layer.astype(jnp.int32)[None]
    embed = functools.partial(embed_rows, layer_arg, planes, w1, embed_w2, gain, lat_rows)
    grid_out = embed(0, 24)
    grid_out = embed(24, 24, grid_out)
    send = sender_latents(pick, planes, from_up, from_down, from_left, from_right, w1, embed_w2, gain)
    live = jnp.stack([live_count, (layer * share).astype(jnp.int32)])
    sums, degree = edge_sums(
        live, near, near_all, arrived, send, edge_w1, edge_b1[:, None], edge_w2,
        message_gain[:, None], message_bias[:, None], node_count,
    )
    parts = lax.all_to_all(sums.reshape(layers, shard_rows, node_count), "gz", 0, 0, tiled=True)
    grid_out = embed(48, 16, grid_out)
    totals = parts.astype(jnp.float32).sum(axis=0)
    result = mesh_own.astype(jnp.float32) + totals / jnp.maximum(degree[:1], 1.0)
    return (result.astype(jnp.bfloat16).reshape(shard_rows, 1, 1, node_count), grid_out)


def solution(mesh):
    return jax.shard_map(
        on_device,
        mesh=mesh,
        in_specs=(
            P(None, "gx", "gy"),
            P(),
            P(),
            P(),
            P(),
            P(),
            P(),
            P(),
            P(),
            P(),
            P("gz", "gx", "gy", None),
            P("gz", "gx", "gy", None),
            P("gx", "gy", None),
            P("gx", "gy", None),
            P("gx", "gy"),
        ),
        out_specs=(P("gz", "gx", "gy", None), P("gz", "gx", "gy")),
        check_vma=False,
    )
```

time: 137 us -> 85.6 us (0.62)
  Pallas kernels: 0 us -> 41.1 us
  other arithmetic: 31.9 us -> 5.63 us
  local copies, waits for them, and re-layouts: 35.5 us -> 12.2 us
  matrix products: 21.9 us -> 0 us
  waiting for transfers between devices: 18.9 us -> 3.44 us
  starting transfers between devices: 26.2 us -> 20.6 us
    pallas_call x0 -> x7, Pallas kernels: none -> 41.1 us  [the longest x3 19.2 us: embed_rows(): pl.pallas_call(functools.partial(embed_kernel, chunk=chunk), name='embed'...]
    dot_general x6 -> x0, matrix products: 21.9 us -> none  [the longest x1 14.6 us: embed_cells(): jnp.dot(embed_w2, grid_hidden, preferred_element_type=jnp.float32)]
    gather x3 -> x0, local copies, waits for them, and re-layouts: 14.2 us -> none  [the longest x1 7.91 us: advance_full(): grid_cols = jnp.take(pad_flat, my_grid, axis=1)]
    all_to_all x3 -> x2, waiting for transfers between devices: 12.7 us -> 0.01 us  [the longest x1 0.01 us: on_device(): lax.all_to_all(outgoing, 'gz', 0, 0, tiled=True)]
    unnamed x34 -> x25, local copies, waits for them, and re-layouts: 15.5 us -> 3.24 us
    concatenate x1, other arithmetic: 12.1 us -> 0.95 us  [on_device(): jnp.concatenate([shares, jnp.broadcast_to(mesh_own[None], (layers, shard_...]
    reduce_sum x4 -> x1, other arithmetic: 10.2 us -> 0.03 us  [on_device(): totals = parts.astype(jnp.float32).sum(axis=0)]
    all_to_all x3 -> x2, starting transfers between devices: 19.1 us -> 14.5 us  [the longest x1 7.56 us: on_device(): lax.all_to_all(outgoing, 'gz', 0, 0, tiled=True)]
  transfers between devices with their start and end apart: 7 -> 6, of which waited for: 3 -> 2; matrix products, arithmetic and copies ran while one was open for 30% -> 14% of each run, Pallas kernels for 0% -> 43%
where the time goes in v1:
time: 85.6 us; the launch traced here: 84.5 us
  Pallas kernels  41.1 us (48%)
  starting transfers between devices  20.6 us (24%)
  local copies, waits for them, and re-layouts  12.2 us (14%)
  other arithmetic  5.63 us (7%)
  waiting for transfers between devices  3.44 us (4%)
  between operations  1.46 us (2%)
    pallas_call x3, Pallas kernels, embed_rows(): pl.pallas_call(functools.partial(embed_kernel, chunk=chunk), name='embed'...  19.2 us
    pallas_call x1, Pallas kernels, planes_of(): pl.pallas_call(planes_kernel, name='planes', grid=(rows // block,), in_sp...  7.58 us
    all_to_all x1, starting transfers between devices, on_device(): lax.all_to_all(outgoing, 'gz', 0, 0, tiled=True)  7.56 us
    all_to_all x1, starting transfers between devices, on_device(): lax.all_to_all(sums.reshape(layers, shard_rows, node_count), 'gz', 0, 0,...  6.93 us
    pallas_call x1, Pallas kernels, sender_latents(): pl.pallas_call(sender_kernel, name='senders', out_shape=jax.ShapeDtypeStr...  6.79 us
    ppermute x4, starting transfers between devices, shifted(): lax.ppermute(value, axis, [(i, (i + by) % size) for i in range(size)])  6.07 us
    pallas_call x1, Pallas kernels, edge_sums(): pl.pallas_call(edge_kernel, name='edges', in_specs=[pl.BlockSpec(memory_s...  5.06 us
    ppermute x4, waiting for transfers between devices, shifted(): lax.ppermute(value, axis, [(i, (i + by) % size) for i in range(size)])  3.44 us
  transfers between devices with their start and end apart: 6, of which 2 were waited for; matrix products, arithmetic and copies ran while one was open for 14% of the time, Pallas kernels for 43%

profile of v1, /device:TPU:32, one launch (start us, length us, event | category | flops | bytes accessed | tf_op | source)
XLA Modules:
  0.0 84.5 jit_solution(3399311475885420793)
XLA Ops:
  0.6 1.5 %reshape_squeeze.3 = bf16[128,4,512]{2,1,0:T(4,128)(2,1)S(1)} reshape(bf16[128,1,1,2048]{3,0,2,1:T(8,128)(2,1)} %param.26) | data formatting | bytes 1048576 | tf_op jit(solution)/shard_map/reshape;squeeze | solution.py:304
  2.2 1.0 %pad_maximum_fusion = bf16[4,128,768]{2,1,0:T(8,128)(2,1)} fusion(bf16[4,128,256]{2,1,0:T(8,128)(2,1)S(1)} %broadcast_in_dim.27, bf16[4,128,512]{2,1,0:T(8,128)(2,1)S(1)} %bitcast.42), kind=kLoop, calls=%fused_computation | loop fusion | flops 1572864 | bytes 1572864 | tf_op jit(solution)/shard_map/concatenate | solution.py:305
  3.2 7.6 %all-to-all-start = ((bf16[4,128,768]{2,1,0:T(8,128)(2,1)}), bf16[4,128,768]{2,1,0:T(8,128)(2,1)S(1)}, u32[]{:S(2)}, u32[]{:S(2)}) async-start(bf16[4,128,768]{2,1,0:T(8,128)(2,1)} %pad_maximum_fusion), calls=%async_computation | async-start | bytes 1572864 | tf_op jit(solution)/shard_map/all_to_all | solution.py:308
  10.8 7.6 %planes.1 = (bf16[192,8192]{1,0:T(8,128)(2,1)}, bf16[192,512]{1,0:T(8,128)(2,1)}, bf16[192,512]{1,0:T(8,128)(2,1)}) custom-call(bf16[186,64,128]{2,1,0:T(8,128)(2,1)} %x_ref.1), custom_call_target="tpu_custom_call" | custom-call | tf_op jit(solution)/shard_map/planes/pallas_call | solution.py:69
  18.3 1.2 %fusion.9 = (bf16[192,1024]{1,0:T(8,128)(2,1)S(1)}, bf16[192,1024]{1,0:T(8,128)(2,1)S(1)}) fusion(bf16[192,8192]{1,0:T(8,128)(2,1)} %get-tuple-element.9.x_ref), kind=kLoop, calls=%fused_computation.37 | loop fusion | bytes 1572864 | tf_op jit(solution)/shard_map/slice | solution.py:313
  19.5 1.9 %collective-permute-start.1 = (bf16[192,1024]{1,0:T(8,128)(2,1)S(1)}, bf16[192,1024]{1,0:T(8,128)(2,1)S(1)}, u32[]{:S(2)}, u32[]{:S(2)}) collective-permute-start(bf16[192,1024]{1,0:T(8,128)(2,1)S(1)} %get-tuple-element.16), channel_id=1, source_target_pairs={{0,224},{32,0},{64,32},{96,64},{128,96},{160,128},{192,160},{224,1... | collective-permute-start | bytes 1179656 | tf_op jit(solution)/shard_map/ppermute | solution.py:269
  23.2 0.7 broadcast_multiply_fusion.w1_ref
  24.5 1.3 %and_select_fusion.1.pick_ref = s32[1,512]{1,0:T(1,128)} fusion(s32[1,1,2048]{2,1,0:T(1,128)} %param.27, s32[]{:T(128)S(6)} %select_n.102, s32[]{:T(128)S(6)} %mul.93, s32[]{:T(128)S(6)} %mul.92), kind=kLoop, calls=%fused_computation.11 | loop fusion | flops 32768 | bytes 4108 | tf_op jit(solution)/shard_map/jit(_where)/select_n | solution.py:332
  26.8 3.1 %collective-permute-done.up_ref = bf16[192,1024]{1,0:T(8,128)(2,1)S(1)} collective-permute-done((bf16[192,1024]{1,0:T(8,128)(2,1)S(1)}, bf16[192,1024]{1,0:T(8,128)(2,1)S(1)}, u32[]{:S(2)}, u32[]{:S(2)}) %collective-permute-start) | collective-permute-done | bytes 393248 | tf_op jit(solution)/shard_map/ppermute | solution.py:269
  29.9 0.8 copy-done.2
  30.7 2.5 %corners.1 = (bf16[192,640]{1,0:T(8,128)(2,1)}, bf16[192,640]{1,0:T(8,128)(2,1)}) custom-call(bf16[192,1024]{1,0:T(8,128)(2,1)} %copy-done.2, bf16[192,1024]{1,0:T(8,128)(2,1)} %copy-done.1, bf16[192,512]{1,0:T(8,128)(2,1)} %get-tuple-element.10.left_in, bf16[192,512]{1,0:T(8,128)(2,1)} %get-tuple-element.11.right_in), custom_call_target="tpu_custom_call" | custom-call | tf_op jit(solution)/shard_map/corners/pallas_call | solution.py:110
  33.1 1.6 %collective-permute-start.2 = (bf16[192,640]{1,0:T(8,128)(2,1)}, bf16[192,640]{1,0:T(8,128)(2,1)S(1)}, u32[]{:S(2)}, u32[]{:S(2)}) collective-permute-start(bf16[192,640]{1,0:T(8,128)(2,1)} %get-tuple-element.12), channel_id=1, source_target_pairs={{0,4},{4,8},{8,12},{12,16},{16,20},{20,24},{24,28},{28,0},{1,5},{5... | collective-permute-start | bytes 737288 | tf_op jit(solution)/shard_map/ppermute | solution.py:269
  34.7 2.6 %collective-permute-start.3 = (bf16[192,640]{1,0:T(8,128)(2,1)}, bf16[192,640]{1,0:T(8,128)(2,1)S(1)}, u32[]{:S(2)}, u32[]{:S(2)}) collective-permute-start(bf16[192,640]{1,0:T(8,128)(2,1)} %get-tuple-element.13), channel_id=1, source_target_pairs={{0,28},{4,0},{8,4},{12,8},{16,12},{20,16},{24,20},{28,24},{1,29},{... | collective-permute-start | bytes 737288 | tf_op jit(solution)/shard_map/ppermute | solution.py:269
  37.9 0.9 %copy.26.gain_ref = f32[512,1]{1,0:T(8,128)} copy(f32[512,1]{0,1:T(1,128)S(1)} %bitcast.47) | data formatting | bytes 4096 | tf_op jit(solution)/shard_map/broadcast_in_dim | solution.py:340
  38.8 0.8 %copy.27.b1_ref = f32[512,1]{1,0:T(8,128)} copy(f32[512,1]{0,1:T(1,128)S(1)} %bitcast.48) | data formatting | bytes 4096 | tf_op jit(solution)/shard_map/broadcast_in_dim | solution.py:348
  39.6 1.5 %copy.28.gain_ref = f32[512,1]{1,0:T(8,128)} copy(f32[512,1]{0,1:T(1,128)} %bitcast.49) | data formatting | bytes 4096 | tf_op jit(solution)/shard_map/broadcast_in_dim | solution.py:349
  41.2 1.6 %copy.29.bias_ref = f32[512,1]{1,0:T(8,128)} copy(f32[512,1]{0,1:T(1,128)} %bitcast.50) | data formatting | bytes 4096 | tf_op jit(solution)/shard_map/broadcast_in_dim | solution.py:349
  42.7 6.9 %embed.3.rest_0_ = bf16[128,64,128]{2,1,0:T(8,128)(2,1)} custom-call(s32[1]{0:T(128)} %bitcast.15.layer_ref, bf16[192,8192]{1,0:T(8,128)(2,1)} %get-tuple-element.9.x_ref, bf16[512,192]{1,0:T(8,128)(2,1)} %broadcast_multiply_fusion.w1_ref, bf16[512,512]{1,0:T(8,128)(2,1)} %wd.5, bf16[512,512]{1,0:T(8,128)(2,1)} %wd.5, bf16[512,512]{1,0:T(8,128)(2,1)} %wd.5, ...), custom_call_target="tpu_custom_call" | custom-call | flops 2415919104 | bytes 1966080 | tf_op jit(solution)/shard_map/embed/pallas_call | solution.py:151
  51.1 6.8 %senders.1.send_ref = bf16[512,512]{1,0:T(8,128)(2,1)} custom-call(s32[1,512]{1,0:T(1,128)} %and_select_fusion.1.pick_ref, bf16[192,8192]{1,0:T(8,128)(2,1)} %get-tuple-element.9.x_ref, bf16[192,1024]{1,0:T(8,128)(2,1)} %copy-done.2, bf16[192,1024]{1,0:T(8,128)(2,1)} %copy-done.1, bf16[192,640]{1,0:T(8,128)(2,1)} %copy-done.10, bf16[192,640]{1,0:T(8,128)(2,1)} %copy-done.11, ...), custom_call_target="tpu_custom_call" | custom-call | flops 3019898880 | bytes 4608000 | tf_op jit(solution)/shard_map/senders/pallas_call | solution.py:199
  57.9 0.9 %copy-done = bf16[4,128,768]{2,1,0:T(8,128)(2,1)} copy-done((bf16[4,128,768]{2,1,0:T(8,128)(2,1)}, bf16[4,128,768]{2,1,0:T(8,128)(2,1)S(1)}, u32[]{:S(2)}) %copy-start) | copy-done | bytes 786456
  58.8 5.1 %edges.1 = (bf16[512,256]{1,0:T(8,128)(2,1)}, f32[8,256]{1,0:T(8,128)}) custom-call(s32[2]{0:T(128)} %pad_add_fusion.live_ref, s32[1,512]{1,0:T(1,128)} %dynamic-slice_bitcast_fusion.near_ref, s32[1,2048]{1,0:T(1,128)} %fusion.10.all_near_ref, bf16[512,768]{1,0:T(8,128)(2,1)} %bitcast.43, bf16[512,512]{1,0:T(8,128)(2,1)} %senders.1.send_ref, ...), custom_call_target="tpu_custom_call" | custom-call | flops 1342177280 | bytes 4194304 | tf_op jit(solution)/shard_map/edges/pallas_call | solution.py:241
  63.8 6.9 %all-to-all-start.1 = ((bf16[4,128,256]{2,1,0:T(8,128)(2,1)}), bf16[4,128,256]{2,1,0:T(8,128)(2,1)S(1)}, u32[]{:S(2)}, u32[]{:S(2)}) async-start(bf16[4,128,256]{2,1,0:T(8,128)(2,1)} %bitcast.44), calls=%async_computation.1 | async-start | bytes 524288 | tf_op jit(solution)/shard_map/all_to_all | solution.py:351
  70.8 7.0 %embed.4.rest_0_ = bf16[128,64,128]{2,1,0:T(8,128)(2,1)} custom-call(s32[1]{0:T(128)} %bitcast.15.layer_ref, bf16[192,8192]{1,0:T(8,128)(2,1)} %get-tuple-element.9.x_ref, bf16[512,192]{1,0:T(8,128)(2,1)} %broadcast_multiply_fusion.w1_ref, bf16[512,512]{1,0:T(8,128)(2,1)} %wd.5, bf16[512,512]{1,0:T(8,128)(2,1)} %wd.5, ...), custom_call_target="tpu_custom_call", output_to_operand_aliasing={{}: (8, {})} | custom-call | flops 2415919104 | bytes 1966080 | tf_op jit(solution)/shard_map/embed/pallas_call | solution.py:151
  77.7 5.3 %embed.5 = bf16[128,64,128]{2,1,0:T(8,128)(2,1)} custom-call(s32[1]{0:T(128)} %bitcast.15.layer_ref, bf16[192,8192]{1,0:T(8,128)(2,1)} %get-tuple-element.9.x_ref, bf16[512,192]{1,0:T(8,128)(2,1)} %broadcast_multiply_fusion.w1_ref, bf16[512,512]{1,0:T(8,128)(2,1)} %wd.5, bf16[512,512]{1,0:T(8,128)(2,1)} %wd.5, ...), custom_call_target="tpu_custom_call", output_to_operand_aliasing={{}: (8, {})} | custom-call | flops 1610612736 | bytes 1310720 | tf_op jit(solution)/shard_map/embed/pallas_call | solution.py:151
  (45 shorter events, 6.1 us)
Async XLA Ops:
  0.6 1.6 %copy-start.3 = (bf16[128,1,1,256]{3,0,2,1:T(8,128)(2,1)S(1)}, bf16[128,1,1,256]{3,0,2,1:T(8,128)(2,1)}, u32[]{:S(2)}) copy-start(bf16[128,1,1,256]{3,0,2,1:T(8,128)(2,1)} %param.25) | copy-start | bytes 196612
  3.2 54.7 %all-to-all-start = ((bf16[4,128,768]{2,1,0:T(8,128)(2,1)}), bf16[4,128,768]{2,1,0:T(8,128)(2,1)S(1)}, u32[]{:S(2)}, u32[]{:S(2)}) async-start(bf16[4,128,768]{2,1,0:T(8,128)(2,1)} %pad_maximum_fusion), calls=%async_computation | async-start | bytes 1572864 | tf_op jit(solution)/shard_map/all_to_all | solution.py:308
  10.8 11.4 %copy-start.9 = (f32[512]{0:T(512)S(1)}, f32[512]{0:T(512)}, u32[]{:S(2)}) copy-start(f32[512]{0:T(512)} %param.17) | copy-start | bytes 6148
  10.8 11.8 %copy-start.5 = (bf16[512,186]{0,1:T(8,128)(2,1)S(1)}, bf16[512,186]{0,1:T(8,128)(2,1)}, u32[]{:S(2)}) copy-start(bf16[512,186]{0,1:T(8,128)(2,1)} %param.16) | copy-start | bytes 571396
  18.3 5.7 %copy-start.6 = (s32[1,1,2048]{2,1,0:T(1,128)S(1)}, s32[1,1,2048]{2,1,0:T(1,128)}, u32[]{:S(2)}) copy-start(s32[1,1,2048]{2,1,0:T(1,128)} %param.28) | copy-start | bytes 24580
  19.5 18.4 %copy-start.7 = (f32[512]{0:T(512)S(1)}, f32[512]{0:T(512)}, u32[]{:S(2)}) copy-start(f32[512]{0:T(512)} %param.19) | copy-start | bytes 6148
  19.5 7.2 %collective-permute-start.1 = (bf16[192,1024]{1,0:T(8,128)(2,1)S(1)}, bf16[192,1024]{1,0:T(8,128)(2,1)S(1)}, u32[]{:S(2)}, u32[]{:S(2)}) collective-permute-start(bf16[192,1024]{1,0:T(8,128)(2,1)S(1)} %get-tuple-element.16), channel_id=1, source_target_pairs={{0,224},{32,0},{64,32},{96,64},{128,96},{160,128},{192,160},{224,1... | collective-permute-start | bytes 1179656 | tf_op jit(solution)/shard_map/ppermute | solution.py:269
  21.5 8.4 %collective-permute-start = (bf16[192,1024]{1,0:T(8,128)(2,1)S(1)}, bf16[192,1024]{1,0:T(8,128)(2,1)S(1)}, u32[]{:S(2)}, u32[]{:S(2)}) collective-permute-start(bf16[192,1024]{1,0:T(8,128)(2,1)S(1)} %get-tuple-element.17), channel_id=1, source_target_pairs={{0,32},{32,64},{64,96},{96,128},{128,160},{160,192},{192,224},{224... | collective-permute-start | bytes 1179656 | tf_op jit(solution)/shard_map/ppermute | solution.py:269
  22.3 16.5 %copy-start.8 = (f32[512]{0:T(512)S(1)}, f32[512]{0:T(512)}, u32[]{:S(2)}) copy-start(f32[512]{0:T(512)} %param.21) | copy-start | bytes 6148
  26.8 3.1 %copy-start.1 = (bf16[192,1024]{1,0:T(8,128)(2,1)}, bf16[192,1024]{1,0:T(8,128)(2,1)S(1)}, u32[]{:S(2)}) copy-start(bf16[192,1024]{1,0:T(8,128)(2,1)S(1)} %collective-permute-done.1.down_ref) | copy-start | bytes 1179652
  29.9 0.8 copy-start.2
  33.1 16.5 %collective-permute-start.2 = (bf16[192,640]{1,0:T(8,128)(2,1)}, bf16[192,640]{1,0:T(8,128)(2,1)S(1)}, u32[]{:S(2)}, u32[]{:S(2)}) collective-permute-start(bf16[192,640]{1,0:T(8,128)(2,1)} %get-tuple-element.12), channel_id=1, source_target_pairs={{0,4},{4,8},{8,12},{12,16},{16,20},{20,24},{24,28},{28,0},{1,5},{5... | collective-permute-start | bytes 737288 | tf_op jit(solution)/shard_map/ppermute | solution.py:269
  34.7 15.0 %collective-permute-start.3 = (bf16[192,640]{1,0:T(8,128)(2,1)}, bf16[192,640]{1,0:T(8,128)(2,1)S(1)}, u32[]{:S(2)}, u32[]{:S(2)}) collective-permute-start(bf16[192,640]{1,0:T(8,128)(2,1)} %get-tuple-element.13), channel_id=1, source_target_pairs={{0,28},{4,0},{8,4},{12,8},{16,12},{20,16},{24,20},{28,24},{1,29},{... | collective-permute-start | bytes 737288 | tf_op jit(solution)/shard_map/ppermute | solution.py:269
  49.7 0.7 copy-start.10
  50.4 0.7 copy-start.11
  57.9 0.9 %copy-start = (bf16[4,128,768]{2,1,0:T(8,128)(2,1)}, bf16[4,128,768]{2,1,0:T(8,128)(2,1)S(1)}, u32[]{:S(2)}) copy-start(bf16[4,128,768]{2,1,0:T(8,128)(2,1)S(1)} %all-to-all-done) | copy-start | bytes 2359300
  63.8 19.9 %all-to-all-start.1 = ((bf16[4,128,256]{2,1,0:T(8,128)(2,1)}), bf16[4,128,256]{2,1,0:T(8,128)(2,1)S(1)}, u32[]{:S(2)}, u32[]{:S(2)}) async-start(bf16[4,128,256]{2,1,0:T(8,128)(2,1)} %bitcast.44), calls=%async_computation.1 | async-start | bytes 524288 | tf_op jit(solution)/shard_map/all_to_all | solution.py:351
  77.7 6.1 %copy-start.4 = (bf16[128,1,1,256]{3,0,2,1:T(8,128)(2,1)S(1)}, bf16[128,1,1,256]{3,0,2,1:T(8,128)(2,1)}, u32[]{:S(2)}) copy-start(bf16[128,1,1,256]{3,0,2,1:T(8,128)(2,1)} %param.25) | copy-start | bytes 196612

commit v2 on v0

v2 whole, which is shorter than its diff:
```python
import functools

import jax
import jax.numpy as jnp
from jax import lax
from jax.experimental import pallas as pl
from jax.experimental.pallas import tpu as pltpu
from jax.sharding import PartitionSpec as P


HALO = 8
LANES = 128
DEPTH = 192
ONES = 3
CHUNK = 16

epsilon = 1e-05


def normalized(values):
    scale = 1.0 / values.shape[0]
    average = jnp.sum(values, axis=0, keepdims=True) * scale
    centred = values - average
    spread = jnp.sum(centred * centred, axis=0, keepdims=True) * scale
    return average, lax.rsqrt(spread + epsilon)


def silu_of_half(half):
    return (half + half * jnp.tanh(half)).astype(jnp.bfloat16)


def dot(a, b):
    return jnp.dot(a, b, preferred_element_type=jnp.float32)


VMEM = pl.BlockSpec(memory_space=pltpu.VMEM)
HBM = pl.BlockSpec(memory_space=pltpu.HBM)


def on_chip(value):
    return pltpu.with_memory_space_constraint(value, pltpu.VMEM)


def off_chip(value):
    return pltpu.with_memory_space_constraint(value, pltpu.HBM)


WIDE = HALO * LANES
VECTORS = 4
EARLY = 40


def column(late_ref, begin, count, latent, which):
    at = latent + 2 * LANES
    parts = [
        late_ref[pl.ds(begin, count), at + n * VECTORS + which : at + n * VECTORS + which + 1].astype(jnp.float32)
        for n in range(ONES)
    ]
    return parts[0] + parts[1] + parts[2]


def plane_group(early_ref, late_ref, g):
    k = g - EARLY // HALO
    return early_ref[g * DEPTH : (g + 1) * DEPTH, :] if k < 0 else late_ref[k * DEPTH : (k + 1) * DEPTH, :]


def three_parts(value):
    parts = []
    for _ in range(ONES):
        part = value.astype(jnp.bfloat16).astype(jnp.float32)
        parts.append(part)
        value = value - part
    return parts


def prepare_kernel(x_ref, w1_ref, b1_ref, gain_ref, edge_b1_ref, message_gain_ref, message_bias_ref, w2_ref,
                   edge_ref, mesh_ref, early_ref, late_ref, top_ref, low_ref, *rest):
    going_refs = rest[:-11]
    (x_in, w1_in, vectors_in, edge_in, mesh_in, in_sem, early_sem, weight_sem, edge_sem, going_sem, out_sem) = rest[-11:]
    channels, rows, lanes = x_ref.shape
    latent = w2_ref.shape[0]
    group = CHUNK
    steps = DEPTH // group
    low = (rows - EARLY) // HALO * DEPTH
    end = low + latent
    sources = [w1_ref, b1_ref, gain_ref, edge_b1_ref, message_gain_ref, message_bias_ref]
    targets = [w1_in] + [vectors_in.at[n] for n in range(5)]
    early = [pltpu.make_async_copy(s, t, early_sem.at[n]) for n, (s, t) in enumerate(zip(sources, targets))]
    for copy in early:
        copy.start()
    incoming = []
    for k in range(steps):
        size = min(group, channels - k * group)
        copy = pltpu.make_async_copy(
            x_ref.at[pl.ds(k * group, size)], x_in.at[pl.ds(k * group, size)], in_sem.at[k]
        )
        copy.start()
        incoming.append(copy)
    layers = len(going_refs) + 1
    _, joined = going_refs[0].shape
    share = edge_in.shape[1] // layers
    layer = lax.axis_index("gz")
    features = [
        pltpu.make_async_copy(edge_ref, edge_in, edge_sem.at[0]),
        pltpu.make_async_copy(mesh_ref, mesh_in, edge_sem.at[1]),
    ]
    for copy in features:
        copy.start()
    weight = pltpu.make_async_copy(w2_ref, late_ref.at[pl.ds(low, latent), pl.ds(0, latent)], weight_sem)
    weight.start()
    for copy in early:
        copy.wait()
    stacked = []
    split = [three_parts(vectors_in[n]) for n in range(1, 1 + VECTORS)]
    for n in range(ONES):
        stacked += [parts[n] for parts in split]
    stacked.append(jnp.zeros((lanes - len(stacked), latent), jnp.float32))
    at = latent + 2 * lanes
    late_ref[low:end, at : at + lanes] = jnp.transpose(jnp.concatenate(stacked, axis=0)).astype(jnp.bfloat16)
    bias = three_parts(vectors_in[0]) + [jnp.zeros((DEPTH - channels - ONES, latent), jnp.float32)]
    full = jnp.concatenate([w1_in[...].astype(jnp.float32)] + bias, axis=0) * 0.5
    late_ref[low:end, latent : latent + DEPTH] = jnp.transpose(full).astype(jnp.bfloat16)

    for copy in features:
        copy.wait()
    going = []
    for j, target in enumerate(going_refs):
        first = pl.multiple_of((layer + j + 1) % layers * share, share)
        pair = [
            (edge_in.at[:, pl.ds(first, share)], target.at[:, pl.ds(0, share)]),
            (mesh_in, target.at[:, pl.ds(share, joined - share)]),
        ]
        going += [pltpu.make_async_copy(s, t, going_sem.at[2 * j + n]) for n, (s, t) in enumerate(pair)]
    for copy in going:
        copy.start()

    row_ids = lax.broadcasted_iota(jnp.int32, (group, lanes), 0)
    for k in range(steps):
        incoming[k].wait()
        cells = jnp.swapaxes(x_in[k * group : (k + 1) * group], 0, 1)
        for r in range(rows):
            plane = cells[r]
            if (k + 1) * group > channels:
                ids = row_ids + k * group
                wide = plane.astype(jnp.float32)
                wide = jnp.where(ids < channels, wide, jnp.where(ids < channels + ONES, 1.0, 0.0))
                plane = wide.astype(jnp.bfloat16)
            target, row = (early_ref, r) if r < EARLY else (late_ref, r - EARLY)
            down = row // HALO * DEPTH + k * group
            over = r % HALO * lanes
            target[down : down + group, over : over + lanes] = plane
    ends = [
        pltpu.make_async_copy(early_ref.at[pl.ds(0, DEPTH), :], top_ref, out_sem.at[0]),
        pltpu.make_async_copy(late_ref.at[pl.ds(low - DEPTH, DEPTH), :], low_ref, out_sem.at[1]),
    ]
    for copy in ends:
        copy.start()
    for copy in [weight] + going + ends:
        copy.wait()


def prepare(grid_inputs, w1, b1, gain, edge_b1, message_gain, message_bias, w2, edge_own, mesh_own, layers):
    channels, rows, lanes = grid_inputs.shape
    latent = w1.shape[0]
    steps = DEPTH // CHUNK
    shard, slots = edge_own.shape
    strip = pltpu.HBM((DEPTH, WIDE), jnp.bfloat16)
    vectors = [a[None] for a in (b1, gain, edge_b1, message_gain, message_bias)]
    return pl.pallas_call(
        prepare_kernel,
        name="prepare",
        compiler_params=pltpu.CompilerParams(vmem_limit_bytes=24 << 20),
        in_specs=[HBM] * 10,
        out_specs=[VMEM, VMEM] + [HBM] * (layers + 1),
        out_shape=[
            pltpu.VMEM((EARLY // HALO * DEPTH, WIDE), jnp.bfloat16),
            pltpu.VMEM(((rows - EARLY) // HALO * DEPTH + latent, WIDE), jnp.bfloat16),
            strip,
            strip,
        ] + [pltpu.HBM((shard, slots // layers + mesh_own.shape[1]), jnp.bfloat16)] * (layers - 1),
        scratch_shapes=[
            pltpu.VMEM((DEPTH, rows, lanes), jnp.bfloat16),
            pltpu.VMEM((channels, latent), jnp.bfloat16),
            pltpu.VMEM((5, 1, latent), jnp.float32),
            pltpu.VMEM(edge_own.shape, jnp.bfloat16),
            pltpu.VMEM(mesh_own.shape, jnp.bfloat16),
            pltpu.SemaphoreType.DMA((steps,)),
            pltpu.SemaphoreType.DMA((6,)),
            pltpu.SemaphoreType.DMA,
            pltpu.SemaphoreType.DMA((2,)),
            pltpu.SemaphoreType.DMA((2 * layers - 2,)),
            pltpu.SemaphoreType.DMA((2,)),
        ],
    )(*[off_chip(a) for a in [grid_inputs, w1.T] + vectors + [w2, edge_own, mesh_own]])


def corners_kernel(early_ref, late_ref, up_ref, down_ref, left_ref, right_ref, *, rows):
    lanes = LANES
    per = lanes // HALO
    lane_ids = lax.broadcasted_iota(jnp.int32, (DEPTH, lanes), 1)
    for r in range(rows + 2 * HALO):
        over = r % HALO * lanes
        if r < rows:
            plane = plane_group(early_ref, late_ref, r // HALO)[:, over : over + lanes]
        else:
            plane = (up_ref if r < rows + HALO else down_ref)[:, over : over + lanes]
        plane = plane.astype(jnp.float32)
        first = r % per * HALO
        again = (first + HALO) % lanes
        mine = (lane_ids >= first) & (lane_ids < first + HALO)
        moved = pltpu.roll(plane, first, 1) if first else plane
        moved_too = pltpu.roll(plane, again, 1) if again else plane
        left = moved if r % per == 0 else jnp.where(mine, moved, left)
        right = moved_too if r % per == 0 else jnp.where(mine, moved_too, right)
        if r % per == per - 1:
            place = slice(r // per * lanes, (r // per + 1) * lanes)
            left_ref[:, place] = left.astype(jnp.bfloat16)
            right_ref[:, place] = right.astype(jnp.bfloat16)


def corners(early, late, up, down, rows):
    packed = pltpu.VMEM((DEPTH, (rows + 2 * HALO) * HALO), jnp.bfloat16)
    return pl.pallas_call(
        functools.partial(corners_kernel, rows=rows),
        name="corners",
        compiler_params=pltpu.CompilerParams(vmem_limit_bytes=8 << 20),
        in_specs=[VMEM] * 4,
        out_specs=[VMEM] * 2,
        out_shape=[packed, packed],
    )(on_chip(early), on_chip(late), on_chip(up), on_chip(down))


def embed_kernel(x_ref, late_ref, *rest, first, latent):
    out_ref, wide_ref = rest[-2:]
    keep, rows, lanes = out_ref.shape
    layers = latent // keep
    layer = lax.axis_index("gz")
    low = late_ref.shape[0] - latent
    w1 = late_ref[low:, latent : latent + DEPTH]
    begin = lambda k: pl.multiple_of(low + (layer + k) % layers * keep, keep)
    w2 = jnp.concatenate([late_ref[pl.ds(begin(k), keep), :latent] for k in range(layers)], axis=0)
    gain = column(late_ref, begin(0), keep, latent, 0)
    here = pl.multiple_of((pl.program_id(0) + first) * DEPTH, DEPTH)
    hidden = silu_of_half(dot(w1, x_ref[pl.ds(here, DEPTH), :]))
    values = dot(w2, hidden)
    average, factor = normalized(values)
    done = (values[:keep] - average) * factor * gain
    for r in range(rows):
        wide_ref[pl.ds(r, keep, stride=rows), :] = done[:, r * lanes : (r + 1) * lanes]
    out_ref[...] = wide_ref[...].reshape(keep, rows, lanes).astype(jnp.bfloat16)


def embed_rows(early, late, latent, keep, rows_total, first, count, earlier=None):
    begin = first // HALO
    source, start = (early, begin) if first < EARLY else (late, begin - EARLY // HALO)
    args = [on_chip(source), on_chip(late)]
    in_specs = [VMEM] * 2
    aliases = {}
    if earlier is not None:
        args.append(off_chip(earlier))
        in_specs.append(HBM)
        aliases = {2: 0}
    cells = count * LANES
    return pl.pallas_call(
        functools.partial(embed_kernel, first=start, latent=latent),
        name="embed",
        compiler_params=pltpu.CompilerParams(vmem_limit_bytes=24 << 20),
        grid=(count // HALO,),
        in_specs=in_specs,
        out_specs=pl.BlockSpec((keep, HALO, LANES), lambda i: (0, i + begin, 0)),
        scratch_shapes=[pltpu.VMEM((keep * HALO, LANES), jnp.float32)],
        out_shape=jax.ShapeDtypeStruct((keep, rows_total, LANES), jnp.bfloat16),
        input_output_aliases=aliases,
        cost_estimate=pl.CostEstimate(
            flops=2 * cells * latent * (256 + latent), transcendentals=cells * latent, bytes_accessed=cells * 640
        ),
    )(*args)


def edge_kernel(count_ref, senders_ref, receivers_ref, early_ref, late_ref, up_ref, down_ref, left_ref, right_ref, *rest,
                lon_bits, rows, layers):
    piece_refs = rest[: layers - 1]
    edge_ref, mesh_ref, w1_ref, w2_ref = rest[layers - 1 : layers + 3]
    own_ref, *sum_refs, degree_ref = rest[layers + 3 : 2 * layers + 4]
    w1_in, w2_in, arrived, sums, sem = rest[2 * layers + 4 :]
    latent, joined = arrived.shape
    shard, nodes = own_ref.shape
    slots = joined - nodes
    lanes = LANES
    layer = lax.axis_index("gz")
    band = lax.axis_index("gx")
    sector = lax.axis_index("gy")
    start = pl.multiple_of(layer * slots, slots)
    place = lambda j: pl.ds(pl.multiple_of((layer + j) % layers * shard, shard), shard)
    pairs = [
        (edge_ref.at[:, pl.ds(start, slots)], arrived.at[place(0), pl.ds(0, slots)]),
        (mesh_ref, arrived.at[place(0), pl.ds(slots, nodes)]),
        (w1_ref, w1_in),
        (w2_ref, w2_in),
    ]
    copies = [pltpu.make_async_copy(s, t, sem.at[n]) for n, (s, t) in enumerate(pairs)]
    for copy in copies:
        copy.start()
    for j, piece in enumerate(piece_refs):
        arrived[place(layers - 1 - j), :] = piece[...]

    low = late_ref.shape[0] - latent
    vector = lambda n: column(late_ref, low, latent, latent, n)
    cell = senders_ref[:, pl.ds(start, slots)]
    lon_total = 1 << lon_bits
    lat = lax.shift_right_logical(cell, lon_bits) - band * rows
    lon = ((cell & (lon_total - 1)) - sector * lanes + HALO & (lon_total - 1)) - HALO
    own = rows * lanes
    side = (rows + 2 * HALO) * HALO
    at_row = jnp.where(
        lat < 0, own + (lat + HALO) * lanes, jnp.where(lat < rows, lat * lanes, own + WIDE + (lat - rows) * lanes)
    )
    at_side = own + 2 * WIDE + HALO * jnp.where(lat < 0, rows + lat + HALO, jnp.where(lat < rows, lat, lat + HALO))
    pick = jnp.where(
        (lon >= 0) & (lon < lanes), at_row + lon, jnp.where(lon < 0, at_side + lon + HALO, at_side + side + lon - lanes)
    )
    planes = [plane_group(early_ref, late_ref, g) for g in range(rows // HALO)]
    total = jnp.zeros((DEPTH, slots), jnp.float32)
    begin = 0
    for part in planes + [up_ref[...], down_ref[...], left_ref[...], right_ref[...]]:
        size = part.shape[1]
        ids = lax.broadcasted_iota(jnp.int32, (size, slots), 0) + begin
        total = total + dot(part, jnp.where(ids == pick, 1.0, 0.0).astype(jnp.bfloat16))
        begin += size
    hidden = silu_of_half(dot(late_ref[low:, latent : latent + DEPTH], total.astype(jnp.bfloat16)))
    values = dot(late_ref[low:, :latent], hidden)
    average, factor = normalized(values)
    send = ((values - average) * factor * vector(0)).astype(jnp.bfloat16)

    tile = band * lax.axis_size("gy") + sector
    live = count_ref[0, 0]
    nt = (((1,), (1,)), ((), ()))
    every = receivers_ref.shape[1]
    slot_all = lax.broadcasted_iota(jnp.int32, (1, every), 1)
    near_all = jnp.where(slot_all < live, receivers_ref[...] - tile * nodes, -1)
    node_all = lax.broadcasted_iota(jnp.int32, (nodes, every), 0)
    counted_all = jnp.where(node_all == near_all, 1.0, 0.0).astype(jnp.bfloat16)
    degree_ref[...] = lax.dot_general(
        jnp.ones((8, every), jnp.bfloat16), counted_all, nt, preferred_element_type=jnp.float32
    )
    near = receivers_ref[:, pl.ds(start, slots)] - tile * nodes
    node_ids = lax.broadcasted_iota(jnp.int32, (nodes, slots), 0)
    onehot = jnp.where(node_ids == near, 1.0, 0.0).astype(jnp.bfloat16)
    slot_ids = lax.broadcasted_iota(jnp.int32, (1, slots), 1) + start
    counted = jnp.where(node_ids == jnp.where(slot_ids < live, near, -1), 1.0, 0.0).astype(jnp.bfloat16)
    for copy in copies:
        copy.wait()
    edge = arrived[:, :slots]
    mesh_cols = dot(arrived[:, slots:], onehot).astype(jnp.bfloat16)
    stacked = jnp.concatenate([edge, send, mesh_cols], axis=0)
    hidden = silu_of_half(0.5 * (dot(w1_in[...], stacked) + vector(1)))
    second = dot(w2_in[...], hidden)
    average, factor = normalized(second)
    message = edge.astype(jnp.float32) + (second - average) * factor * vector(2) + vector(3)
    sums[...] = lax.dot_general(message.astype(jnp.bfloat16), counted, nt, preferred_element_type=jnp.float32)
    own_ref[...] = sums[place(0), :]
    for j, target in enumerate(sum_refs):
        target[...] = sums[place(j + 1), :].astype(jnp.bfloat16)


def edge_sums(count, senders, receivers, early, late, up, down, left, right, pieces, edge_own, mesh_own, w1, w2,
              rows, lon_total):
    latent = w2.shape[0]
    layers = len(pieces) + 1
    shard, nodes = mesh_own.shape
    slots = edge_own.shape[1] // layers
    near_by = [on_chip(a) for a in (early, late, up, down, left, right, *pieces)]
    far = [off_chip(a) for a in (edge_own, mesh_own, w1, w2)]
    return pl.pallas_call(
        functools.partial(edge_kernel, lon_bits=lon_total.bit_length() - 1, rows=rows, layers=layers),
        name="edges",
        compiler_params=pltpu.CompilerParams(vmem_limit_bytes=32 << 20),
        in_specs=[pl.BlockSpec(memory_space=pltpu.SMEM)] + [VMEM] * (2 + len(near_by)) + [HBM] * 4,
        out_specs=[VMEM] * (layers + 1),
        out_shape=[pltpu.VMEM((shard, nodes), jnp.float32)]
        + [pltpu.VMEM((shard, nodes), jnp.bfloat16)] * (layers - 1)
        + [pltpu.VMEM((8, nodes), jnp.float32)],
        scratch_shapes=[
            pltpu.VMEM(w1.shape, jnp.bfloat16),
            pltpu.VMEM(w2.shape, jnp.bfloat16),
            pltpu.VMEM((latent, slots + nodes), jnp.bfloat16),
            pltpu.VMEM((latent, nodes), jnp.float32),
            pltpu.SemaphoreType.DMA((4,)),
        ],
        cost_estimate=pl.CostEstimate(flops=6 * 10**9, transcendentals=0, bytes_accessed=1 << 22),
    )(count, senders, receivers, *near_by, *far)


def finish_kernel(own_ref, *rest):
    *part_refs, degree_ref, mesh_ref, out_ref = rest
    totals = own_ref[...]
    for part in part_refs:
        totals = totals + part[...].astype(jnp.float32)
    scale = jnp.maximum(degree_ref[0:1, :], 1.0)
    out_ref[...] = (mesh_ref[...].astype(jnp.float32) + totals / scale).astype(jnp.bfloat16)


def finish(own, parts, degree, mesh_own):
    args = [on_chip(a) for a in (own, *parts, degree, mesh_own)]
    return pl.pallas_call(
        finish_kernel,
        name="finish",
        compiler_params=pltpu.CompilerParams(vmem_limit_bytes=8 << 20),
        in_specs=[VMEM] * len(args),
        out_specs=VMEM,
        out_shape=jax.ShapeDtypeStruct(mesh_own.shape, jnp.bfloat16),
    )(*args)


def shifted(value, axis, by):
    size = lax.axis_size(axis)
    return lax.ppermute(value, axis, [(i, (i + by) % size) for i in range(size)])


def on_device(
    grid_inputs,
    embed_w1,
    embed_b1,
    embed_w2,
    embed_gain,
    edge_w1,
    edge_b1,
    edge_w2,
    message_gain,
    message_bias,
    mesh_latent,
    edge_latent,
    senders,
    receivers,
    edge_counts,
):
    latent = embed_w2.shape[0]
    shard_rows = mesh_latent.shape[0]
    lat_rows, lon_cols = grid_inputs.shape[1:]
    node_count = mesh_latent.shape[3]
    layers = lax.axis_size("gz")
    lon_total = lon_cols * lax.axis_size("gy")
    mesh_own = mesh_latent[:, 0, 0, :]
    edge_own = edge_latent[:, 0, 0, :]

    early, late, top, low, *outgoing = prepare(
        grid_inputs, embed_w1, embed_b1, embed_gain, edge_b1, message_gain, message_bias, embed_w2, edge_own, mesh_own,
        layers,
    )
    embed = functools.partial(embed_rows, early, late, latent, shard_rows, lat_rows)
    from_up = shifted(low, "gx", 1)
    from_down = shifted(top, "gx", -1)
    pieces = [shifted(piece, "gz", j + 1) for j, piece in enumerate(outgoing)]
    grid_out = embed(0, 16)
    from_up, from_down, grid_out = lax.optimization_barrier((from_up, from_down, grid_out))
    left, right = corners(early, late, from_up, from_down, lat_rows)
    from_left = shifted(right, "gy", 1)
    from_right = shifted(left, "gy", -1)
    grid_out = embed(16, EARLY - 16, grid_out)
    from_left, from_right, grid_out = lax.optimization_barrier((from_left, from_right, grid_out))
    own, *sums, degree = edge_sums(
        edge_counts, senders[0], receivers[0], early, late, from_up, from_down, from_left, from_right, pieces,
        edge_own, mesh_own, edge_w1, edge_w2, lat_rows, lon_total,
    )
    parts = [shifted(part, "gz", j + 1) for j, part in enumerate(sums)]
    grid_out = embed(EARLY, lat_rows - EARLY, grid_out)
    *parts, grid_out = lax.optimization_barrier((*parts, grid_out))
    result = finish(own, parts, degree, mesh_own)
    return (result.reshape(shard_rows, 1, 1, node_count), grid_out)


def solution(mesh):
    return jax.shard_map(
        on_device,
        mesh=mesh,
        in_specs=(
            P(None, "gx", "gy"),
            P(),
            P(),
            P(),
            P(),
            P(),
            P(),
            P(),
            P(),
            P(),
            P("gz", "gx", "gy", None),
            P("gz", "gx", "gy", None),
            P("gx", "gy", None),
            P("gx", "gy", None),
            P("gx", "gy"),
        ),
        out_specs=(P("gz", "gx", "gy", None), P("gz", "gx", "gy")),
        check_vma=False,
    )
```

time: 137 us -> 67.9 us (0.50)
  local copies, waits for them, and re-layouts: 35.5 us -> 0.03 us
  other arithmetic: 31.9 us -> 0 us
  Pallas kernels: 0 us -> 27 us
  matrix products: 21.9 us -> 0 us
  waiting for transfers between devices: 18.9 us -> 12.6 us
    pallas_call x0 -> x7, Pallas kernels: none -> 27 us  [the longest x3 12.8 us: embed_rows(): pl.pallas_call(functools.partial(embed_kernel, first=start, latent=latent...]
    dot_general x6 -> x0, matrix products: 21.9 us -> none  [the longest x1 14.6 us: embed_cells(): jnp.dot(embed_w2, grid_hidden, preferred_element_type=jnp.float32)]
    ppermute x4 -> x10, starting transfers between devices: 7.09 us -> 26.2 us  [shifted(): lax.ppermute(value, axis, [(i, (i + by) % size) for i in range(size)])]
    all_to_all x3 -> x0, starting transfers between devices: 19.1 us -> none  [the longest x1 7.56 us: on_device(): lax.all_to_all(arranged, 'gz', split_axis=2, concat_axis=0, tiled=True)]
    unnamed x34 -> x12, local copies, waits for them, and re-layouts: 15.5 us -> 0.03 us
    gather x3 -> x0, local copies, waits for them, and re-layouts: 14.2 us -> none  [the longest x1 7.91 us: advance_full(): grid_cols = jnp.take(pad_flat, my_grid, axis=1)]
    all_to_all x3 -> x0, waiting for transfers between devices: 12.7 us -> none  [the longest x1 11 us: sum_at_owner(): lax.all_to_all(pieces, axis, split_axis=0, concat_axis=0, tiled=True)]
    concatenate x1 -> x0, other arithmetic: 12.1 us -> none  [padded_2(): value = jnp.concatenate([before, value, after], axis=dim)]
  transfers between devices with their start and end apart: 7 -> 10, of which waited for: 3 -> 3; matrix products, arithmetic and copies ran while one was open for 30% -> 0% of each run, Pallas kernels for 0% -> 19%
where the time goes in v2:
time: 67.9 us; the launch traced here: 67.2 us
  Pallas kernels  27 us (40%)
  starting transfers between devices  26.2 us (39%)
  waiting for transfers between devices  12.6 us (19%)
  between operations  1.36 us (2%)
    ppermute x10, starting transfers between devices, shifted(): lax.ppermute(value, axis, [(i, (i + by) % size) for i in range(size)])  26.2 us
    pallas_call x3, Pallas kernels, embed_rows(): pl.pallas_call(functools.partial(embed_kernel, first=start, latent=latent...  12.8 us
    ppermute x10, waiting for transfers between devices, shifted(): lax.ppermute(value, axis, [(i, (i + by) % size) for i in range(size)])  12.6 us
    pallas_call x1, Pallas kernels, edge_sums(): pl.pallas_call(functools.partial(edge_kernel, lon_bits=lon_total.bit_leng...  7.22 us
    pallas_call x1, Pallas kernels, prepare(): pl.pallas_call(prepare_kernel, name='prepare', compiler_params=pltpu.Comp...  4.19 us
    pallas_call x1, Pallas kernels, corners(): pl.pallas_call(functools.partial(corners_kernel, rows=rows), name='corner...  2.14 us
  transfers between devices with their start and end apart: 10, of which 3 were waited for; matrix products, arithmetic and copies ran while one was open for 0% of the time, Pallas kernels for 19%

profile of v2, /device:TPU:32, one launch (start us, length us, event | category | flops | bytes accessed | tf_op | source)
XLA Modules:
  0.0 67.2 jit_solution(11038504398927168730)
XLA Ops:
  0.6 4.2 %prepare.1 = (bf16[960,1024]{1,0:T(8,128)(2,1)S(1)}, bf16[1088,1024]{1,0:T(8,128)(2,1)S(1)}, bf16[192,1024]{1,0:T(8,128)(2,1)}, bf16[192,1024]{1,0:T(8,128)(2,1)...) custom-call(bf16[186,64,128]{2,1,0:T(8,128)(2,1)} %x_ref.1, ...), custom_call_target="tpu_custom_call" | custom-call | tf_op jit(solution)/shard_map/prepare/pallas_call | solution.py:169
  4.8 0.0 collective-permute-start
  4.9 2.9 %collective-permute-start.1 = (bf16[192,1024]{1,0:T(8,128)(2,1)}, bf16[192,1024]{1,0:T(8,128)(2,1)S(1)}, u32[]{:S(2)}, u32[]{:S(2)}) collective-permute-start(bf16[192,1024]{1,0:T(8,128)(2,1)} %get-tuple-element.29), channel_id=1, source_target_pairs={{0,224},{32,0},{64,32},{96,64},{128,96},{160,128},{192,160},{224,1... | collective-permute-start | bytes 1179656 | tf_op jit(solution)/shard_map/ppermute | solution.py:417
  7.8 3.4 %embed.3.rest_0_ = bf16[128,64,128]{2,1,0:T(8,128)(2,1)} custom-call(bf16[960,1024]{1,0:T(8,128)(2,1)S(1)} %get-tuple-element.26.x_ref.early_ref, bf16[1088,1024]{1,0:T(8,128)(2,1)S(1)} %get-tuple-element.27.late_ref.x_ref), custom_call_target="tpu_custom_call" | custom-call | flops 1610612736 | bytes 1310720 | tf_op jit(solution)/shard_map/embed/pallas_call | solution.py:264
  11.2 2.3 %collective-permute-done.up_ref = bf16[192,1024]{1,0:T(8,128)(2,1)S(1)} collective-permute-done((bf16[192,1024]{1,0:T(8,128)(2,1)}, bf16[192,1024]{1,0:T(8,128)(2,1)S(1)}, u32[]{:S(2)}, u32[]{:S(2)}) %collective-permute-start) | collective-permute-done | bytes 393248 | tf_op jit(solution)/shard_map/ppermute | solution.py:417
  13.5 0.0 collective-permute-done.1.down_ref
  13.5 2.1 %corners.1 = (bf16[192,640]{1,0:T(8,128)(2,1)S(1)}, bf16[192,640]{1,0:T(8,128)(2,1)S(1)}) custom-call(bf16[960,1024]{1,0:T(8,128)(2,1)S(1)} %get-tuple-element.26.x_ref.early_ref, bf16[1088,1024]{1,0:T(8,128)(2,1)S(1)} %get-tuple-element.27.late_ref.x_ref, bf16[192,1024]{1,0:T(8,128)(2,1)S(1)} %collective-permute-done.up_ref, ...), custom_call_target="tpu_custom_call" | custom-call | tf_op jit(solution)/shard_map/corners/pallas_call | solution.py:223
  15.6 1.7 %collective-permute-start.2 = (bf16[192,640]{1,0:T(8,128)(2,1)S(1)}, bf16[192,640]{1,0:T(8,128)(2,1)S(1)}, u32[]{:S(2)}, u32[]{:S(2)}) collective-permute-start(bf16[192,640]{1,0:T(8,128)(2,1)S(1)} %get-tuple-element.32), channel_id=1, source_target_pairs={{0,4},{4,8},{8,12},{12,16},{16,20},{20,24},{24,28},{28,0},{1,5},{5... | collective-permute-start | bytes 737288 | tf_op jit(solution)/shard_map/ppermute | solution.py:417
  17.3 2.6 %collective-permute-start.3 = (bf16[192,640]{1,0:T(8,128)(2,1)S(1)}, bf16[192,640]{1,0:T(8,128)(2,1)S(1)}, u32[]{:S(2)}, u32[]{:S(2)}) collective-permute-start(bf16[192,640]{1,0:T(8,128)(2,1)S(1)} %get-tuple-element.33), channel_id=1, source_target_pairs={{0,28},{4,0},{8,4},{12,8},{16,12},{20,16},{24,20},{28,24},{1,29},{... | collective-permute-start | bytes 737288 | tf_op jit(solution)/shard_map/ppermute | solution.py:417
  19.8 3.3 %collective-permute-start.4 = (bf16[128,768]{1,0:T(8,128)(2,1)S(1)}, bf16[128,768]{1,0:T(8,128)(2,1)S(1)}, u32[]{:S(2)}, u32[]{:S(2)}) collective-permute-start(bf16[128,768]{1,0:T(8,128)(2,1)S(1)} %copy-done.5), channel_id=1, source_target_pairs={{0,1},{1,2},{2,3},{3,0},{4,5},{5,6},{6,7},{7,4},{8,9},{9,10},{10,1... | collective-permute-start | bytes 589832 | tf_op jit(solution)/shard_map/ppermute | solution.py:417
  23.1 4.5 %collective-permute-start.5 = (bf16[128,768]{1,0:T(8,128)(2,1)S(1)}, bf16[128,768]{1,0:T(8,128)(2,1)S(1)}, u32[]{:S(2)}, u32[]{:S(2)}) collective-permute-start(bf16[128,768]{1,0:T(8,128)(2,1)S(1)} %copy-done.4), channel_id=1, source_target_pairs={{0,2},{1,3},{2,0},{3,1},{4,6},{5,7},{6,4},{7,5},{8,10},{9,11},{10,... | collective-permute-start | bytes 589832 | tf_op jit(solution)/shard_map/ppermute | solution.py:417
  27.6 2.7 %collective-permute-start.6 = (bf16[128,768]{1,0:T(8,128)(2,1)S(1)}, bf16[128,768]{1,0:T(8,128)(2,1)S(1)}, u32[]{:S(2)}, u32[]{:S(2)}) collective-permute-start(bf16[128,768]{1,0:T(8,128)(2,1)S(1)} %copy-done.3), channel_id=1, source_target_pairs={{0,3},{1,0},{2,1},{3,2},{4,7},{5,4},{6,5},{7,6},{8,11},{9,8},{10,9... | collective-permute-start | bytes 589832 | tf_op jit(solution)/shard_map/ppermute | solution.py:417
  30.9 0.0 copy-start.1
  30.9 0.0 copy-start.2
  30.9 4.7 %embed.4.rest_0_ = bf16[128,64,128]{2,1,0:T(8,128)(2,1)} custom-call(bf16[960,1024]{1,0:T(8,128)(2,1)S(1)} %get-tuple-element.26.x_ref.early_ref, bf16[1088,1024]{1,0:T(8,128)(2,1)S(1)} %get-tuple-element.27.late_ref.x_ref, bf16[128,64,128]{2,1,0:T(8,128)(2,1)} %embed.3.rest_0_), custom_call_target="tpu_custom_call", output_to_operand_aliasing={{}: (2, {})} | custom-call | flops 2415919104 | bytes 1966080 | tf_op jit(solution)/shard_map/embed/pallas_call | solution.py:264
  35.7 0.0 collective-permute-done.2.left_ref
  35.7 9.6 %collective-permute-done.5.rest_1_ = bf16[128,768]{1,0:T(8,128)(2,1)S(1)} collective-permute-done((bf16[128,768]{1,0:T(8,128)(2,1)S(1)}, bf16[128,768]{1,0:T(8,128)(2,1)S(1)}, u32[]{:S(2)}, u32[]{:S(2)}) %collective-permute-start.5) | collective-permute-done | bytes 196640 | tf_op jit(solution)/shard_map/ppermute | solution.py:417
  45.3 0.6 collective-permute-done.6.rest_2_
  45.9 7.2 %edges.1 = (f32[128,256]{1,0:T(8,128)S(1)}, bf16[128,256]{1,0:T(8,128)(2,1)S(1)}, bf16[128,256]{1,0:T(8,128)(2,1)S(1)}, bf16[128,256]{1,0:T(8,128)(2,1)S(1)}, f32[8,256]{1,0:T(8,128)S(1)}) custom-call(s32[1,1]{1,0:T(1,128)S(6)} %copy.21.count_ref, s32[1,2048]{1,0:T(1,128)S(1)} %bitcast.14, s32[1,2048]{1,0:T(1,128)S(1)} %bitcast.15, ...), custom_call_target="tpu_custom_call" | custom-call | flops 6000000000 | bytes 4194304 | tf_op jit(solution)/shard_map/edges/pallas_call | solution.py:374
  53.1 3.6 %collective-permute-start.7 = (bf16[128,256]{1,0:T(8,128)(2,1)S(1)}, bf16[128,256]{1,0:T(8,128)(2,1)S(1)}, u32[]{:S(2)}, u32[]{:S(2)}) collective-permute-start(bf16[128,256]{1,0:T(8,128)(2,1)S(1)} %get-tuple-element.41), channel_id=1, source_target_pairs={{0,1},{1,2},{2,3},{3,0},{4,5},{5,6},{6,7},{7,4},{8,9},{9,10},{10,1... | collective-permute-start | bytes 196616 | tf_op jit(solution)/shard_map/ppermute | solution.py:417
  56.8 1.5 %collective-permute-start.8 = (bf16[128,256]{1,0:T(8,128)(2,1)S(1)}, bf16[128,256]{1,0:T(8,128)(2,1)S(1)}, u32[]{:S(2)}, u32[]{:S(2)}) collective-permute-start(bf16[128,256]{1,0:T(8,128)(2,1)S(1)} %get-tuple-element.42), channel_id=1, source_target_pairs={{0,2},{1,3},{2,0},{3,1},{4,6},{5,7},{6,4},{7,5},{8,10},{9,11},{10,... | collective-permute-start | bytes 196616 | tf_op jit(solution)/shard_map/ppermute | solution.py:417
  58.3 3.5 %collective-permute-start.9 = (bf16[128,256]{1,0:T(8,128)(2,1)S(1)}, bf16[128,256]{1,0:T(8,128)(2,1)S(1)}, u32[]{:S(2)}, u32[]{:S(2)}) collective-permute-start(bf16[128,256]{1,0:T(8,128)(2,1)S(1)} %get-tuple-element.43), channel_id=1, source_target_pairs={{0,3},{1,0},{2,1},{3,2},{4,7},{5,4},{6,5},{7,6},{8,11},{9,8},{10,9... | collective-permute-start | bytes 196616 | tf_op jit(solution)/shard_map/ppermute | solution.py:417
  61.8 4.7 %embed.5 = bf16[128,64,128]{2,1,0:T(8,128)(2,1)} custom-call(bf16[1088,1024]{1,0:T(8,128)(2,1)S(1)} %get-tuple-element.27.late_ref.x_ref, bf16[1088,1024]{1,0:T(8,128)(2,1)S(1)} %get-tuple-element.27.late_ref.x_ref, bf16[128,64,128]{2,1,0:T(8,128)(2,1)} %embed.4.rest_0_), custom_call_target="tpu_custom_call", output_to_operand_aliasing={{}: (2, {})} | custom-call | flops 2415919104 | bytes 1966080 | tf_op jit(solution)/shard_map/embed/pallas_call | solution.py:264
  66.5 0.7 %finish.1 = bf16[128,256]{1,0:T(8,128)(2,1)} custom-call(f32[128,256]{1,0:T(8,128)S(1)} %get-tuple-element.40.own_ref, bf16[128,256]{1,0:T(8,128)(2,1)S(1)} %collective-permute-done.7.rest_0_, bf16[128,256]{1,0:T(8,128)(2,1)S(1)} %collective-permute-done.8.rest_1_, bf16[128,256]{1,0:T(8,128)(2,1)S(1)} %collective-permute-done.9.rest_2_, ...), custom_call_target="tpu_custom_call" | custom-call | tf_op jit(solution)/shard_map/finish/pallas_call | solution.py:405
  (15 shorter events, 0.0 us)
Async XLA Ops:
  4.8 8.6 %collective-permute-start = (bf16[192,1024]{1,0:T(8,128)(2,1)}, bf16[192,1024]{1,0:T(8,128)(2,1)S(1)}, u32[]{:S(2)}, u32[]{:S(2)}) collective-permute-start(bf16[192,1024]{1,0:T(8,128)(2,1)} %get-tuple-element.28), channel_id=1, source_target_pairs={{0,32},{32,64},{64,96},{96,128},{128,160},{160,192},{192,224},{224... | collective-permute-start | bytes 1179656 | tf_op jit(solution)/shard_map/ppermute | solution.py:417
  4.9 8.6 %collective-permute-start.1 = (bf16[192,1024]{1,0:T(8,128)(2,1)}, bf16[192,1024]{1,0:T(8,128)(2,1)S(1)}, u32[]{:S(2)}, u32[]{:S(2)}) collective-permute-start(bf16[192,1024]{1,0:T(8,128)(2,1)} %get-tuple-element.29), channel_id=1, source_target_pairs={{0,224},{32,0},{64,32},{96,64},{128,96},{160,128},{192,160},{224,1... | collective-permute-start | bytes 1179656 | tf_op jit(solution)/shard_map/ppermute | solution.py:417
  11.2 8.7 %copy-start.5 = (bf16[128,768]{1,0:T(8,128)(2,1)S(1)}, bf16[128,768]{1,0:T(8,128)(2,1)}, u32[]{:S(2)}) copy-start(bf16[128,768]{1,0:T(8,128)(2,1)} %get-tuple-element.37) | copy-start | bytes 589828
  11.2 12.0 %copy-start.4 = (bf16[128,768]{1,0:T(8,128)(2,1)S(1)}, bf16[128,768]{1,0:T(8,128)(2,1)}, u32[]{:S(2)}) copy-start(bf16[128,768]{1,0:T(8,128)(2,1)} %get-tuple-element.38) | copy-start | bytes 589828
  11.2 16.4 %copy-start.3 = (bf16[128,768]{1,0:T(8,128)(2,1)S(1)}, bf16[128,768]{1,0:T(8,128)(2,1)}, u32[]{:S(2)}) copy-start(bf16[128,768]{1,0:T(8,128)(2,1)} %get-tuple-element.39) | copy-start | bytes 589828
  15.6 20.0 %collective-permute-start.2 = (bf16[192,640]{1,0:T(8,128)(2,1)S(1)}, bf16[192,640]{1,0:T(8,128)(2,1)S(1)}, u32[]{:S(2)}, u32[]{:S(2)}) collective-permute-start(bf16[192,640]{1,0:T(8,128)(2,1)S(1)} %get-tuple-element.32), channel_id=1, source_target_pairs={{0,4},{4,8},{8,12},{12,16},{16,20},{20,24},{24,28},{28,0},{1,5},{5... | collective-permute-start | bytes 737288 | tf_op jit(solution)/shard_map/ppermute | solution.py:417
  17.3 18.4 %collective-permute-start.3 = (bf16[192,640]{1,0:T(8,128)(2,1)S(1)}, bf16[192,640]{1,0:T(8,128)(2,1)S(1)}, u32[]{:S(2)}, u32[]{:S(2)}) collective-permute-start(bf16[192,640]{1,0:T(8,128)(2,1)S(1)} %get-tuple-element.33), channel_id=1, source_target_pairs={{0,28},{4,0},{8,4},{12,8},{16,12},{20,16},{24,20},{28,24},{1,29},{... | collective-permute-start | bytes 737288 | tf_op jit(solution)/shard_map/ppermute | solution.py:417
  19.8 15.8 %collective-permute-start.4 = (bf16[128,768]{1,0:T(8,128)(2,1)S(1)}, bf16[128,768]{1,0:T(8,128)(2,1)S(1)}, u32[]{:S(2)}, u32[]{:S(2)}) collective-permute-start(bf16[128,768]{1,0:T(8,128)(2,1)S(1)} %copy-done.5), channel_id=1, source_target_pairs={{0,1},{1,2},{2,3},{3,0},{4,5},{5,6},{6,7},{7,4},{8,9},{9,10},{10,1... | collective-permute-start | bytes 589832 | tf_op jit(solution)/shard_map/ppermute | solution.py:417
  23.1 22.2 %collective-permute-start.5 = (bf16[128,768]{1,0:T(8,128)(2,1)S(1)}, bf16[128,768]{1,0:T(8,128)(2,1)S(1)}, u32[]{:S(2)}, u32[]{:S(2)}) collective-permute-start(bf16[128,768]{1,0:T(8,128)(2,1)S(1)} %copy-done.4), channel_id=1, source_target_pairs={{0,2},{1,3},{2,0},{3,1},{4,6},{5,7},{6,4},{7,5},{8,10},{9,11},{10,... | collective-permute-start | bytes 589832 | tf_op jit(solution)/shard_map/ppermute | solution.py:417
  27.6 18.3 %collective-permute-start.6 = (bf16[128,768]{1,0:T(8,128)(2,1)S(1)}, bf16[128,768]{1,0:T(8,128)(2,1)S(1)}, u32[]{:S(2)}, u32[]{:S(2)}) collective-permute-start(bf16[128,768]{1,0:T(8,128)(2,1)S(1)} %copy-done.3), channel_id=1, source_target_pairs={{0,3},{1,0},{2,1},{3,2},{4,7},{5,4},{6,5},{7,6},{8,11},{9,8},{10,9... | collective-permute-start | bytes 589832 | tf_op jit(solution)/shard_map/ppermute | solution.py:417
  30.9 15.0 %copy-start.1 = (s32[1,1,2048]{2,1,0:T(1,128)S(1)}, s32[1,1,2048]{2,1,0:T(1,128)}, u32[]{:S(2)}) copy-start(s32[1,1,2048]{2,1,0:T(1,128)} %param.27) | copy-start | bytes 24580
  30.9 15.0 %copy-start.2 = (s32[1,1,2048]{2,1,0:T(1,128)S(1)}, s32[1,1,2048]{2,1,0:T(1,128)}, u32[]{:S(2)}) copy-start(s32[1,1,2048]{2,1,0:T(1,128)} %param.28) | copy-start | bytes 24580
  53.1 13.3 %collective-permute-start.7 = (bf16[128,256]{1,0:T(8,128)(2,1)S(1)}, bf16[128,256]{1,0:T(8,128)(2,1)S(1)}, u32[]{:S(2)}, u32[]{:S(2)}) collective-permute-start(bf16[128,256]{1,0:T(8,128)(2,1)S(1)} %get-tuple-element.41), channel_id=1, source_target_pairs={{0,1},{1,2},{2,3},{3,0},{4,5},{5,6},{6,7},{7,4},{8,9},{9,10},{10,1... | collective-permute-start | bytes 196616 | tf_op jit(solution)/shard_map/ppermute | solution.py:417
  56.8 9.7 %collective-permute-start.8 = (bf16[128,256]{1,0:T(8,128)(2,1)S(1)}, bf16[128,256]{1,0:T(8,128)(2,1)S(1)}, u32[]{:S(2)}, u32[]{:S(2)}) collective-permute-start(bf16[128,256]{1,0:T(8,128)(2,1)S(1)} %get-tuple-element.42), channel_id=1, source_target_pairs={{0,2},{1,3},{2,0},{3,1},{4,6},{5,7},{6,4},{7,5},{8,10},{9,11},{10,... | collective-permute-start | bytes 196616 | tf_op jit(solution)/shard_map/ppermute | solution.py:417
  58.3 8.2 %copy-start = (bf16[128,1,1,256]{3,0,2,1:T(8,128)(2,1)S(1)}, bf16[128,1,1,256]{3,0,2,1:T(8,128)(2,1)}, u32[]{:S(2)}) copy-start(bf16[128,1,1,256]{3,0,2,1:T(8,128)(2,1)} %param.25) | copy-start | bytes 196612
  58.3 8.2 %collective-permute-start.9 = (bf16[128,256]{1,0:T(8,128)(2,1)S(1)}, bf16[128,256]{1,0:T(8,128)(2,1)S(1)}, u32[]{:S(2)}, u32[]{:S(2)}) collective-permute-start(bf16[128,256]{1,0:T(8,128)(2,1)S(1)} %get-tuple-element.43), channel_id=1, source_target_pairs={{0,3},{1,0},{2,1},{3,2},{4,7},{5,4},{6,5},{7,6},{8,11},{9,8},{10,9... | collective-permute-start | bytes 196616 | tf_op jit(solution)/shard_map/ppermute | solution.py:417

commit v3 on v2

--- a/solution.py
+++ b/solution.py
@@ -47,7 +47,7 @@
 
 WIDE = HALO * LANES
 VECTORS = 4
-EARLY = 40
+EARLY = 32
 
 
 def column(late_ref, begin, count, latent, which):
@@ -164,20 +164,20 @@
     latent = w1.shape[0]
     steps = DEPTH // CHUNK
     shard, slots = edge_own.shape
-    strip = pltpu.HBM((DEPTH, WIDE), jnp.bfloat16)
+    strip = pltpu.VMEM((DEPTH, WIDE), jnp.bfloat16)
     vectors = [a[None] for a in (b1, gain, edge_b1, message_gain, message_bias)]
     return pl.pallas_call(
         prepare_kernel,
         name="prepare",
         compiler_params=pltpu.CompilerParams(vmem_limit_bytes=24 << 20),
         in_specs=[HBM] * 10,
-        out_specs=[VMEM, VMEM] + [HBM] * (layers + 1),
+        out_specs=[VMEM] * (layers + 3),
         out_shape=[
             pltpu.VMEM((EARLY // HALO * DEPTH, WIDE), jnp.bfloat16),
             pltpu.VMEM(((rows - EARLY) // HALO * DEPTH + latent, WIDE), jnp.bfloat16),
             strip,
             strip,
-        ] + [pltpu.HBM((shard, slots // layers + mesh_own.shape[1]), jnp.bfloat16)] * (layers - 1),
+        ] + [pltpu.VMEM((shard, slots // layers + mesh_own.shape[1]), jnp.bfloat16)] * (layers - 1),
         scratch_shapes=[
             pltpu.VMEM((DEPTH, rows, lanes), jnp.bfloat16),
             pltpu.VMEM((channels, latent), jnp.bfloat16),
@@ -194,40 +194,129 @@
     )(*[off_chip(a) for a in [grid_inputs, w1.T] + vectors + [w2, edge_own, mesh_own]])
 
 
-def corners_kernel(early_ref, late_ref, up_ref, down_ref, left_ref, right_ref, *, rows):
+def sender_places(senders_ref, slots, rows, lon_bits):
+    lanes = LANES
+    start = pl.multiple_of(lax.axis_index("gz") * slots, slots)
+    cell = senders_ref[:, pl.ds(start, slots)]
+    lon_total = 1 << lon_bits
+    lat = lax.shift_right_logical(cell, lon_bits) - lax.axis_index("gx") * rows
+    lon = ((cell & (lon_total - 1)) - lax.axis_index("gy") * lanes + HALO & (lon_total - 1)) - HALO
+    own = rows * lanes
+    side = (rows + 2 * HALO) * HALO
+    at_row = jnp.where(
+        lat < 0, own + (lat + HALO) * lanes, jnp.where(lat < rows, lat * lanes, own + WIDE + (lat - rows) * lanes)
+    )
+    at_side = own + 2 * WIDE + HALO * jnp.where(lat < 0, rows + lat + HALO, jnp.where(lat < rows, lat, lat + HALO))
+    return jnp.where(
+        (lon >= 0) & (lon < lanes), at_row + lon, jnp.where(lon < 0, at_side + lon + HALO, at_side + side + lon - lanes)
+    )
+
+
+def picked(parts, begin, places, total):
+    slots = places.shape[1]
+    for part in parts:
+        size = part.shape[1]
+        ids = lax.broadcasted_iota(jnp.int32, (size, slots), 0) + begin
+        total = total + dot(part, jnp.where(ids == places, 1.0, 0.0).astype(jnp.bfloat16))
+        begin += size
+    return total
+
+
+def packed_columns(planes, first_row, left_ref, right_ref):
     lanes = LANES
     per = lanes // HALO
     lane_ids = lax.broadcasted_iota(jnp.int32, (DEPTH, lanes), 1)
-    for r in range(rows + 2 * HALO):
-        over = r % HALO * lanes
-        if r < rows:
-            plane = plane_group(early_ref, late_ref, r // HALO)[:, over : over + lanes]
-        else:
-            plane = (up_ref if r < rows + HALO else down_ref)[:, over : over + lanes]
-        plane = plane.astype(jnp.float32)
-        first = r % per * HALO
-        again = (first + HALO) % lanes
-        mine = (lane_ids >= first) & (lane_ids < first + HALO)
-        moved = pltpu.roll(plane, first, 1) if first else plane
-        moved_too = pltpu.roll(plane, again, 1) if again else plane
-        left = moved if r % per == 0 else jnp.where(mine, moved, left)
-        right = moved_too if r % per == 0 else jnp.where(mine, moved_too, right)
-        if r % per == per - 1:
-            place = slice(r // per * lanes, (r // per + 1) * lanes)
-            left_ref[:, place] = left.astype(jnp.bfloat16)
-            right_ref[:, place] = right.astype(jnp.bfloat16)
-
-
-def corners(early, late, up, down, rows):
+    for g, cells in enumerate(planes):
+        for k in range(HALO):
+            r = first_row + g * HALO + k
+            plane = cells[:, k * lanes : (k + 1) * lanes].astype(jnp.float32)
+            first = r % per * HALO
+            again = (first + HALO) % lanes
+            mine = (lane_ids >= first) & (lane_ids < first + HALO)
+            moved = pltpu.roll(plane, first, 1) if first else plane
+            moved_too = pltpu.roll(plane, again, 1) if again else plane
+            left = moved if r % per == 0 else jnp.where(mine, moved, left)
+            right = moved_too if r % per == 0 else jnp.where(mine, moved_too, right)
+            if r % per == per - 1:
+                place = slice(r // per * lanes, (r // per + 1) * lanes)
+                left_ref[:, place] = left.astype(jnp.bfloat16)
+                right_ref[:, place] = right.astype(jnp.bfloat16)
+
+
+def own_kernel(count_ref, senders_ref, receivers_ref, early_ref, late_ref,
+               left_ref, right_ref, picked_ref, near_ref, live_ref, degree_ref, count, sem, *, rows, lon_bits):
+    counting = pltpu.make_async_copy(count_ref, count, sem)
+    counting.start()
+    slots = picked_ref.shape[1]
+    places = sender_places(senders_ref, slots, rows, lon_bits)
+    total = jnp.zeros(picked_ref.shape, jnp.float32)
+    pair = 2
+    for g in range(0, rows // HALO, pair):
+        planes = [plane_group(early_ref, late_ref, g + n) for n in range(pair)]
+        total = picked(planes, g * WIDE, places, total)
+        packed_columns(planes, g * HALO, left_ref, right_ref)
+    picked_ref[...] = total
+
+    counting.wait()
+    live = count[0, 0]
+    nodes = near_ref.shape[0]
+    tile = lax.axis_index("gx") * lax.axis_size("gy") + lax.axis_index("gy")
+    nt = (((1,), (1,)), ((), ()))
+    every = receivers_ref.shape[1]
+    slot_all = lax.broadcasted_iota(jnp.int32, (1, every), 1)
+    near_all = jnp.where(slot_all < live, receivers_ref[...] - tile * nodes, -1)
+    node_all = lax.broadcasted_iota(jnp.int32, (nodes, every), 0)
+    counted_all = jnp.where(node_all == near_all, 1.0, 0.0).astype(jnp.bfloat16)
+    degree_ref[...] = lax.dot_general(
+        jnp.ones((8, every), jnp.bfloat16), counted_all, nt, preferred_element_type=jnp.float32
+    )
+    start = pl.multiple_of(lax.axis_index("gz") * slots, slots)
+    near = receivers_ref[:, pl.ds(start, slots)] - tile * nodes
+    node_ids = lax.broadcasted_iota(jnp.int32, (nodes, slots), 0)
+    near_ref[...] = jnp.where(node_ids == near, 1.0, 0.0).astype(jnp.bfloat16)
+    slot_ids = lax.broadcasted_iota(jnp.int32, (1, slots), 1) + start
+    live_ref[...] = jnp.where(node_ids == jnp.where(slot_ids < live, near, -1), 1.0, 0.0).astype(jnp.bfloat16)
+
+
+def own_work(count, senders, receivers, early, late, rows, slots, nodes, lon_total):
     packed = pltpu.VMEM((DEPTH, (rows + 2 * HALO) * HALO), jnp.bfloat16)
+    table = pltpu.VMEM((nodes, slots), jnp.bfloat16)
     return pl.pallas_call(
-        functools.partial(corners_kernel, rows=rows),
-        name="corners",
-        compiler_params=pltpu.CompilerParams(vmem_limit_bytes=8 << 20),
-        in_specs=[VMEM] * 4,
-        out_specs=[VMEM] * 2,
-        out_shape=[packed, packed],
-    )(on_chip(early), on_chip(late), on_chip(up), on_chip(down))
+        functools.partial(own_kernel, rows=rows, lon_bits=lon_total.bit_length() - 1),
+        name="own",
+        compiler_params=pltpu.CompilerParams(vmem_limit_bytes=32 << 20),
+        in_specs=[pl.BlockSpec(memory_space=pl.ANY)] + [VMEM] * 4,
+        out_specs=[VMEM] * 6,
+        out_shape=[
+            packed,
+            packed,
+            pltpu.VMEM((DEPTH, slots), jnp.float32),
+            table,
+            table,
+            pltpu.VMEM((8, nodes), jnp.float32),
+        ],
+        scratch_shapes=[pltpu.SMEM((1, 1), jnp.int32), pltpu.SemaphoreType.DMA],
+        cost_estimate=pl.CostEstimate(flops=2 * 10**9, transcendentals=0, bytes_accessed=1 << 22),
+    )(count, senders, receivers, on_chip(early), on_chip(late))
+
+
+def strip_kernel(senders_ref, up_ref, down_ref, left_in, right_in, picked_in, left_ref, right_ref, picked_ref, *, rows, lon_bits):
+    strips = [up_ref[...], down_ref[...]]
+    packed_columns(strips, rows, left_ref, right_ref)
+    places = sender_places(senders_ref, picked_ref.shape[1], rows, lon_bits)
+    picked_ref[...] = picked(strips, rows * LANES, places, picked_in[...])
+
+
+def strip_work(senders, up, down, left, right, chosen, rows, lon_total):
+    return pl.pallas_call(
+        functools.partial(strip_kernel, rows=rows, lon_bits=lon_total.bit_length() - 1),
+        name="strips",
+        compiler_params=pltpu.CompilerParams(vmem_limit_bytes=16 << 20),
+        in_specs=[VMEM] * 6,
+        out_specs=[VMEM] * 3,
+        out_shape=[pltpu.VMEM(a.shape, a.dtype) for a in (left, right, chosen)],
+        input_output_aliases={3: 0, 4: 1, 5: 2},
+    )(senders, *[on_chip(a) for a in (up, down, left, right, chosen)])
 
 
 def embed_kernel(x_ref, late_ref, *rest, first, latent):
@@ -277,19 +366,16 @@
     )(*args)
 
 
-def edge_kernel(count_ref, senders_ref, receivers_ref, early_ref, late_ref, up_ref, down_ref, left_ref, right_ref, *rest,
+def edge_kernel(senders_ref, picked_ref, near_ref, live_ref, late_ref, left_ref, right_ref, *rest,
                 lon_bits, rows, layers):
     piece_refs = rest[: layers - 1]
     edge_ref, mesh_ref, w1_ref, w2_ref = rest[layers - 1 : layers + 3]
-    own_ref, *sum_refs, degree_ref = rest[layers + 3 : 2 * layers + 4]
-    w1_in, w2_in, arrived, sums, sem = rest[2 * layers + 4 :]
+    own_ref, *sum_refs = rest[layers + 3 : 2 * layers + 3]
+    w1_in, w2_in, arrived, sums, sem = rest[2 * layers + 3 :]
     latent, joined = arrived.shape
     shard, nodes = own_ref.shape
     slots = joined - nodes
-    lanes = LANES
     layer = lax.axis_index("gz")
-    band = lax.axis_index("gx")
-    sector = lax.axis_index("gy")
     start = pl.multiple_of(layer * slots, slots)
     place = lambda j: pl.ds(pl.multiple_of((layer + j) % layers * shard, shard), shard)
     pairs = [
@@ -306,80 +392,45 @@
 
     low = late_ref.shape[0] - latent
     vector = lambda n: column(late_ref, low, latent, latent, n)
-    cell = senders_ref[:, pl.ds(start, slots)]
-    lon_total = 1 << lon_bits
-    lat = lax.shift_right_logical(cell, lon_bits) - band * rows
-    lon = ((cell & (lon_total - 1)) - sector * lanes + HALO & (lon_total - 1)) - HALO
-    own = rows * lanes
-    side = (rows + 2 * HALO) * HALO
-    at_row = jnp.where(
-        lat < 0, own + (lat + HALO) * lanes, jnp.where(lat < rows, lat * lanes, own + WIDE + (lat - rows) * lanes)
-    )
-    at_side = own + 2 * WIDE + HALO * jnp.where(lat < 0, rows + lat + HALO, jnp.where(lat < rows, lat, lat + HALO))
-    pick = jnp.where(
-        (lon >= 0) & (lon < lanes), at_row + lon, jnp.where(lon < 0, at_side + lon + HALO, at_side + side + lon - lanes)
-    )
-    planes = [plane_group(early_ref, late_ref, g) for g in range(rows // HALO)]
-    total = jnp.zeros((DEPTH, slots), jnp.float32)
-    begin = 0
-    for part in planes + [up_ref[...], down_ref[...], left_ref[...], right_ref[...]]:
-        size = part.shape[1]
-        ids = lax.broadcasted_iota(jnp.int32, (size, slots), 0) + begin
-        total = total + dot(part, jnp.where(ids == pick, 1.0, 0.0).astype(jnp.bfloat16))
-        begin += size
+    sides = [left_ref[...], right_ref[...]]
+    total = picked(sides, (rows + 2 * HALO) * LANES, sender_places(senders_ref, slots, rows, lon_bits), picked_ref[...])
     hidden = silu_of_half(dot(late_ref[low:, latent : latent + DEPTH], total.astype(jnp.bfloat16)))
     values = dot(late_ref[low:, :latent], hidden)
     average, factor = normalized(values)
     send = ((values - average) * factor * vector(0)).astype(jnp.bfloat16)
 
-    tile = band * lax.axis_size("gy") + sector
-    live = count_ref[0, 0]
     nt = (((1,), (1,)), ((), ()))
-    every = receivers_ref.shape[1]
-    slot_all = lax.broadcasted_iota(jnp.int32, (1, every), 1)
-    near_all = jnp.where(slot_all < live, receivers_ref[...] - tile * nodes, -1)
-    node_all = lax.broadcasted_iota(jnp.int32, (nodes, every), 0)
-    counted_all = jnp.where(node_all == near_all, 1.0, 0.0).astype(jnp.bfloat16)
-    degree_ref[...] = lax.dot_general(
-        jnp.ones((8, every), jnp.bfloat16), counted_all, nt, preferred_element_type=jnp.float32
-    )
-    near = receivers_ref[:, pl.ds(start, slots)] - tile * nodes
-    node_ids = lax.broadcasted_iota(jnp.int32, (nodes, slots), 0)
-    onehot = jnp.where(node_ids == near, 1.0, 0.0).astype(jnp.bfloat16)
-    slot_ids = lax.broadcasted_iota(jnp.int32, (1, slots), 1) + start
-    counted = jnp.where(node_ids == jnp.where(slot_ids < live, near, -1), 1.0, 0.0).astype(jnp.bfloat16)
     for copy in copies:
         copy.wait()
     edge = arrived[:, :slots]
-    mesh_cols = dot(arrived[:, slots:], onehot).astype(jnp.bfloat16)
+    mesh_cols = dot(arrived[:, slots:], near_ref[...]).astype(jnp.bfloat16)
     stacked = jnp.concatenate([edge, send, mesh_cols], axis=0)
     hidden = silu_of_half(0.5 * (dot(w1_in[...], stacked) + vector(1)))
     second = dot(w2_in[...], hidden)
     average, factor = normalized(second)
     message = edge.astype(jnp.float32) + (second - average) * factor * vector(2) + vector(3)
-    sums[...] = lax.dot_general(message.astype(jnp.bfloat16), counted, nt, preferred_element_type=jnp.float32)
+    sums[...] = lax.dot_general(message.astype(jnp.bfloat16), live_ref[...], nt, preferred_element_type=jnp.float32)
     own_ref[...] = sums[place(0), :]
     for j, target in enumerate(sum_refs):
         target[...] = sums[place(j + 1), :].astype(jnp.bfloat16)
 
 
-def edge_sums(count, senders, receivers, early, late, up, down, left, right, pieces, edge_own, mesh_own, w1, w2,
+def edge_sums(senders, chosen, near, live, late, left, right, pieces, edge_own, mesh_own, w1, w2,
               rows, lon_total):
     latent = w2.shape[0]
     layers = len(pieces) + 1
     shard, nodes = mesh_own.shape
     slots = edge_own.shape[1] // layers
-    near_by = [on_chip(a) for a in (early, late, up, down, left, right, *pieces)]
+    near_by = [on_chip(a) for a in (chosen, near, live, late, left, right, *pieces)]
     far = [off_chip(a) for a in (edge_own, mesh_own, w1, w2)]
     return pl.pallas_call(
         functools.partial(edge_kernel, lon_bits=lon_total.bit_length() - 1, rows=rows, layers=layers),
         name="edges",
         compiler_params=pltpu.CompilerParams(vmem_limit_bytes=32 << 20),
-        in_specs=[pl.BlockSpec(memory_space=pltpu.SMEM)] + [VMEM] * (2 + len(near_by)) + [HBM] * 4,
-        out_specs=[VMEM] * (layers + 1),
+        in_specs=[VMEM] * (1 + len(near_by)) + [HBM] * 4,
+        out_specs=[VMEM] * layers,
         out_shape=[pltpu.VMEM((shard, nodes), jnp.float32)]
-        + [pltpu.VMEM((shard, nodes), jnp.bfloat16)] * (layers - 1)
-        + [pltpu.VMEM((8, nodes), jnp.float32)],
+        + [pltpu.VMEM((shard, nodes), jnp.bfloat16)] * (layers - 1),
         scratch_shapes=[
             pltpu.VMEM(w1.shape, jnp.bfloat16),
             pltpu.VMEM(w2.shape, jnp.bfloat16),
@@ -387,8 +438,8 @@
             pltpu.VMEM((latent, nodes), jnp.float32),
             pltpu.SemaphoreType.DMA((4,)),
         ],
-        cost_estimate=pl.CostEstimate(flops=6 * 10**9, transcendentals=0, bytes_accessed=1 << 22),
-    )(count, senders, receivers, *near_by, *far)
+        cost_estimate=pl.CostEstimate(flops=4 * 10**9, transcendentals=0, bytes_accessed=1 << 22),
+    )(senders, *near_by, *far)
 
 
 def finish_kernel(own_ref, *rest):
@@ -451,16 +502,19 @@
     from_up = shifted(low, "gx", 1)
     from_down = shifted(top, "gx", -1)
     pieces = [shifted(piece, "gz", j + 1) for j, piece in enumerate(outgoing)]
-    grid_out = embed(0, 16)
-    from_up, from_down, grid_out = lax.optimization_barrier((from_up, from_down, grid_out))
-    left, right = corners(early, late, from_up, from_down, lat_rows)
+    left, right, chosen, near, live, degree = own_work(
+        edge_counts, senders[0], receivers[0], early, late, lat_rows, edge_own.shape[1] // layers, mesh_own.shape[1],
+        lon_total,
+    )
+    from_up, from_down, left, right, chosen = lax.optimization_barrier((from_up, from_down, left, right, chosen))
+    left, right, chosen = strip_work(senders[0], from_up, from_down, left, right, chosen, lat_rows, lon_total)
     from_left = shifted(right, "gy", 1)
     from_right = shifted(left, "gy", -1)
-    grid_out = embed(16, EARLY - 16, grid_out)
-    from_left, from_right, grid_out = lax.optimization_barrier((from_left, from_right, grid_out))
-    own, *sums, degree = edge_sums(
-        edge_counts, senders[0], receivers[0], early, late, from_up, from_down, from_left, from_right, pieces,
-        edge_own, mesh_own, edge_w1, edge_w2, lat_rows, lon_total,
+    grid_out = embed(0, EARLY)
+    from_left, from_right, grid_out, *pieces = lax.optimization_barrier((from_left, from_right, grid_out, *pieces))
+    own, *sums = edge_sums(
+        senders[0], chosen, near, live, late, from_left, from_right, pieces, edge_own, mesh_own, edge_w1, edge_w2,
+        lat_rows, lon_total,
     )
     parts = [shifted(part, "gz", j + 1) for j, part in enumerate(sums)]
     grid_out = embed(EARLY, lat_rows - EARLY, grid_out)

time: 67.9 us -> 57.6 us (0.85)
  the two profiles are of different devices: /device:TPU:32 before, /device:TPU:2 now
where the time goes in v3:
time: 57.6 us; the launch traced here: 57.4 us
  Pallas kernels  25.3 us (44%)
  starting transfers between devices  23.2 us (40%)
  waiting for transfers between devices  7.54 us (13%)
  between operations  1.4 us (2%)
    ppermute x10, starting transfers between devices, shifted(): lax.ppermute(value, axis, [(i, (i + by) % size) for i in range(size)])  23.2 us
    pallas_call x2, Pallas kernels, embed_rows(): pl.pallas_call(functools.partial(embed_kernel, first=start, latent=latent...  12 us
    ppermute x10, waiting for transfers between devices, shifted(): lax.ppermute(value, axis, [(i, (i + by) % size) for i in range(size)])  7.54 us
    pallas_call x1, Pallas kernels, edge_sums(): pl.pallas_call(functools.partial(edge_kernel, lon_bits=lon_total.bit_leng...  4.36 us
    pallas_call x1, Pallas kernels, prepare(): pl.pallas_call(prepare_kernel, name='prepare', compiler_params=pltpu.Comp...  3.86 us
    pallas_call x1, Pallas kernels, own_work(): pl.pallas_call(functools.partial(own_kernel, rows=rows, lon_bits=lon_tota...  3.57 us
  transfers between devices with their start and end apart: 10, of which 1 were waited for; matrix products, arithmetic and copies ran while one was open for 0% of the time, Pallas kernels for 29%

profile of v3, /device:TPU:2, one launch (start us, length us, event | category | flops | bytes accessed | tf_op | source)
XLA Modules:
  0.0 57.4 jit_solution(16987097478571592059)
XLA Ops:
  0.7 3.9 %prepare.1 = (bf16[768,1024]{1,0:T(8,128)(2,1)S(1)}, bf16[1280,1024]{1,0:T(8,128)(2,1)S(1)}, bf16[192,1024]{1,0:T(8,128)(2,1)S(1)}, bf16[192,1024]{1,0:T(8,128)(...) custom-call(bf16[186,64,128]{2,1,0:T(8,128)(2,1)} %x_ref.1, ...), custom_call_target="tpu_custom_call" | custom-call | tf_op jit(solution)/shard_map/prepare/pallas_call | solution.py:169
  4.5 0.0 collective-permute-start
  4.5 1.7 %collective-permute-start.1 = (bf16[192,1024]{1,0:T(8,128)(2,1)S(1)}, bf16[192,1024]{1,0:T(8,128)(2,1)S(1)}, u32[]{:S(2)}, u32[]{:S(2)}) collective-permute-start(bf16[192,1024]{1,0:T(8,128)(2,1)S(1)} %get-tuple-element.38), channel_id=1, source_target_pairs={{0,224},{32,0},{64,32},{96,64},{128,96},{160,128},{192,160},{224,1... | collective-permute-start | bytes 1179656 | tf_op jit(solution)/shard_map/ppermute | solution.py:468
  6.3 3.3 %collective-permute-start.4 = (bf16[128,768]{1,0:T(8,128)(2,1)S(1)}, bf16[128,768]{1,0:T(8,128)(2,1)S(1)}, u32[]{:S(2)}, u32[]{:S(2)}) collective-permute-start(bf16[128,768]{1,0:T(8,128)(2,1)S(1)} %get-tuple-element.54), channel_id=1, source_target_pairs={{0,1},{1,2},{2,3},{3,0},{4,5},{5,6},{6,7},{7,4},{8,9},{9,10},{10,1... | collective-permute-start | bytes 589832 | tf_op jit(solution)/shard_map/ppermute | solution.py:468
  9.6 5.4 %collective-permute-start.5 = (bf16[128,768]{1,0:T(8,128)(2,1)S(1)}, bf16[128,768]{1,0:T(8,128)(2,1)S(1)}, u32[]{:S(2)}, u32[]{:S(2)}) collective-permute-start(bf16[128,768]{1,0:T(8,128)(2,1)S(1)} %get-tuple-element.55), channel_id=1, source_target_pairs={{0,2},{1,3},{2,0},{3,1},{4,6},{5,7},{6,4},{7,5},{8,10},{9,11},{10,... | collective-permute-start | bytes 589832 | tf_op jit(solution)/shard_map/ppermute | solution.py:468
  14.9 2.7 %collective-permute-start.6 = (bf16[128,768]{1,0:T(8,128)(2,1)S(1)}, bf16[128,768]{1,0:T(8,128)(2,1)S(1)}, u32[]{:S(2)}, u32[]{:S(2)}) collective-permute-start(bf16[128,768]{1,0:T(8,128)(2,1)S(1)} %get-tuple-element.56), channel_id=1, source_target_pairs={{0,3},{1,0},{2,1},{3,2},{4,7},{5,4},{6,5},{7,6},{8,11},{9,8},{10,9... | collective-permute-start | bytes 589832 | tf_op jit(solution)/shard_map/ppermute | solution.py:468
  18.3 3.6 %own.1 = (bf16[192,640]{1,0:T(8,128)(2,1)S(1)}, bf16[192,640]{1,0:T(8,128)(2,1)S(1)}, f32[192,512]{1,0:T(8,128)S(1)}, bf16[256,512]{1,0:T(8,128)(2,1)S(1)}, bf16...) custom-call(s32[1,1]{1,0:T(1,128)S(6)} %copy.25.count_ref, s32[1,2048]{1,0:T(1,128)S(1)} %bitcast.14, ...), custom_call_target="tpu_custom_call" | custom-call | flops 2000000000 | bytes 4194304 | tf_op jit(solution)/shard_map/own/pallas_call | solution.py:284
  21.9 0.0 collective-permute-done.up_ref
  21.9 0.0 collective-permute-done.1.down_ref
  21.9 0.8 %strips.1 = (bf16[192,640]{1,0:T(8,128)(2,1)S(1)}, bf16[192,640]{1,0:T(8,128)(2,1)S(1)}, f32[192,512]{1,0:T(8,128)S(1)}) custom-call(s32[1,2048]{1,0:T(1,128)S(1)} %bitcast.15, bf16[192,1024]{1,0:T(8,128)(2,1)S(1)} %collective-permute-done.up_ref, ...), custom_call_target="tpu_custom_call", output_to_operand_aliasing={{0}: (3, {}), {1}: (4, {}), {2}: (5, {})} | custom-call | tf_op jit(solution)/shard_map/strips/pallas_call | solution.py:311
  22.6 1.7 %collective-permute-start.2 = (bf16[192,640]{1,0:T(8,128)(2,1)S(1)}, bf16[192,640]{1,0:T(8,128)(2,1)S(1)}, u32[]{:S(2)}, u32[]{:S(2)}) collective-permute-start(bf16[192,640]{1,0:T(8,128)(2,1)S(1)} %get-tuple-element.52), channel_id=1, source_target_pairs={{0,4},{4,8},{8,12},{12,16},{16,20},{20,24},{24,28},{28,0},{1,5},{5... | collective-permute-start | bytes 737288 | tf_op jit(solution)/shard_map/ppermute | solution.py:468
  24.3 2.6 %collective-permute-start.3 = (bf16[192,640]{1,0:T(8,128)(2,1)S(1)}, bf16[192,640]{1,0:T(8,128)(2,1)S(1)}, u32[]{:S(2)}, u32[]{:S(2)}) collective-permute-start(bf16[192,640]{1,0:T(8,128)(2,1)S(1)} %get-tuple-element.53), channel_id=1, source_target_pairs={{0,28},{4,0},{8,4},{12,8},{16,12},{20,16},{24,20},{28,24},{1,29},{... | collective-permute-start | bytes 737288 | tf_op jit(solution)/shard_map/ppermute | solution.py:468
  26.9 6.0 %embed.2.rest_0_ = bf16[128,64,128]{2,1,0:T(8,128)(2,1)} custom-call(bf16[768,1024]{1,0:T(8,128)(2,1)S(1)} %get-tuple-element.39.early_ref.x_ref, bf16[1280,1024]{1,0:T(8,128)(2,1)S(1)} %get-tuple-element.40.late_ref.x_ref), custom_call_target="tpu_custom_call" | custom-call | flops 3221225472 | bytes 2621440 | tf_op jit(solution)/shard_map/embed/pallas_call | solution.py:353
  32.9 0.0 collective-permute-done.4.rest_0_
  32.9 0.0 collective-permute-done.5.rest_1_
  32.9 0.0 collective-permute-done.6.rest_2_
  32.9 7.5 %collective-permute-done.2.left_ref = bf16[192,640]{1,0:T(8,128)(2,1)S(1)} collective-permute-done((bf16[192,640]{1,0:T(8,128)(2,1)S(1)}, bf16[192,640]{1,0:T(8,128)(2,1)S(1)}, u32[]{:S(2)}, u32[]{:S(2)}) %collective-permute-start.2) | collective-permute-done | bytes 245792 | tf_op jit(solution)/shard_map/ppermute | solution.py:468
  40.4 0.0 collective-permute-done.3.right_ref
  40.4 4.4 %edges.1 = (f32[128,256]{1,0:T(8,128)S(1)}, bf16[128,256]{1,0:T(8,128)(2,1)S(1)}, bf16[128,256]{1,0:T(8,128)(2,1)S(1)}, bf16[128,256]{1,0:T(8,128)(2,1)S(1)}) custom-call(s32[1,2048]{1,0:T(1,128)S(1)} %bitcast.16, f32[192,512]{1,0:T(8,128)S(1)} %get-tuple-element.49.picked_ref, bf16[256,512]{1,0:T(8,128)(2,1)S(1)} %get-tuple-element.50.near_ref, ...), custom_call_target="tpu_custom_call" | custom-call | flops 4000000000 | bytes 4194304 | tf_op jit(solution)/shard_map/edges/pallas_call | solution.py:426
  44.8 0.7 %collective-permute-start.7 = (bf16[128,256]{1,0:T(8,128)(2,1)S(1)}, bf16[128,256]{1,0:T(8,128)(2,1)S(1)}, u32[]{:S(2)}, u32[]{:S(2)}) collective-permute-start(bf16[128,256]{1,0:T(8,128)(2,1)S(1)} %get-tuple-element.63), channel_id=1, source_target_pairs={{0,1},{1,2},{2,3},{3,0},{4,5},{5,6},{6,7},{7,4},{8,9},{9,10},{10,1... | collective-permute-start | bytes 196616 | tf_op jit(solution)/shard_map/ppermute | solution.py:468
  45.5 4.8 %collective-permute-start.8 = (bf16[128,256]{1,0:T(8,128)(2,1)S(1)}, bf16[128,256]{1,0:T(8,128)(2,1)S(1)}, u32[]{:S(2)}, u32[]{:S(2)}) collective-permute-start(bf16[128,256]{1,0:T(8,128)(2,1)S(1)} %get-tuple-element.64), channel_id=1, source_target_pairs={{0,2},{1,3},{2,0},{3,1},{4,6},{5,7},{6,4},{7,5},{8,10},{9,11},{10,... | collective-permute-start | bytes 196616 | tf_op jit(solution)/shard_map/ppermute | solution.py:468
  50.3 0.5 collective-permute-start.9
  50.7 6.0 %embed.3 = bf16[128,64,128]{2,1,0:T(8,128)(2,1)} custom-call(bf16[1280,1024]{1,0:T(8,128)(2,1)S(1)} %get-tuple-element.40.late_ref.x_ref, bf16[1280,1024]{1,0:T(8,128)(2,1)S(1)} %get-tuple-element.40.late_ref.x_ref, bf16[128,64,128]{2,1,0:T(8,128)(2,1)} %embed.2.rest_0_), custom_call_target="tpu_custom_call", output_to_operand_aliasing={{}: (2, {})} | custom-call | flops 3221225472 | bytes 2621440 | tf_op jit(solution)/shard_map/embed/pallas_call | solution.py:353
  56.8 0.7 %finish.1 = bf16[128,256]{1,0:T(8,128)(2,1)} custom-call(f32[128,256]{1,0:T(8,128)S(1)} %get-tuple-element.62.own_ref, bf16[128,256]{1,0:T(8,128)(2,1)S(1)} %collective-permute-done.7.rest_0_, bf16[128,256]{1,0:T(8,128)(2,1)S(1)} %collective-permute-done.8.rest_1_, bf16[128,256]{1,0:T(8,128)(2,1)S(1)} %collective-permute-done.9.rest_2_, ...), custom_call_target="tpu_custom_call" | custom-call | tf_op jit(solution)/shard_map/finish/pallas_call | solution.py:456
  (9 shorter events, 0.0 us)
Async XLA Ops:
  0.6 17.6 %copy-start.1 = (s32[1,1,2048]{2,1,0:T(1,128)S(1)}, s32[1,1,2048]{2,1,0:T(1,128)}, u32[]{:S(2)}) copy-start(s32[1,1,2048]{2,1,0:T(1,128)} %param.27) | copy-start | bytes 24580
  0.6 17.6 %copy-start.2 = (s32[1,1,2048]{2,1,0:T(1,128)S(1)}, s32[1,1,2048]{2,1,0:T(1,128)}, u32[]{:S(2)}) copy-start(s32[1,1,2048]{2,1,0:T(1,128)} %param.28) | copy-start | bytes 24580
  4.5 17.3 %collective-permute-start = (bf16[192,1024]{1,0:T(8,128)(2,1)S(1)}, bf16[192,1024]{1,0:T(8,128)(2,1)S(1)}, u32[]{:S(2)}, u32[]{:S(2)}) collective-permute-start(bf16[192,1024]{1,0:T(8,128)(2,1)S(1)} %get-tuple-element.37), channel_id=1, source_target_pairs={{0,32},{32,64},{64,96},{96,128},{128,160},{160,192},{192,224},{224... | collective-permute-start | bytes 1179656 | tf_op jit(solution)/shard_map/ppermute | solution.py:468
  4.5 17.3 %collective-permute-start.1 = (bf16[192,1024]{1,0:T(8,128)(2,1)S(1)}, bf16[192,1024]{1,0:T(8,128)(2,1)S(1)}, u32[]{:S(2)}, u32[]{:S(2)}) collective-permute-start(bf16[192,1024]{1,0:T(8,128)(2,1)S(1)} %get-tuple-element.38), channel_id=1, source_target_pairs={{0,224},{32,0},{64,32},{96,64},{128,96},{160,128},{192,160},{224,1... | collective-permute-start | bytes 1179656 | tf_op jit(solution)/shard_map/ppermute | solution.py:468
  6.3 26.6 %collective-permute-start.4 = (bf16[128,768]{1,0:T(8,128)(2,1)S(1)}, bf16[128,768]{1,0:T(8,128)(2,1)S(1)}, u32[]{:S(2)}, u32[]{:S(2)}) collective-permute-start(bf16[128,768]{1,0:T(8,128)(2,1)S(1)} %get-tuple-element.54), channel_id=1, source_target_pairs={{0,1},{1,2},{2,3},{3,0},{4,5},{5,6},{6,7},{7,4},{8,9},{9,10},{10,1... | collective-permute-start | bytes 589832 | tf_op jit(solution)/shard_map/ppermute | solution.py:468
  9.6 23.3 %collective-permute-start.5 = (bf16[128,768]{1,0:T(8,128)(2,1)S(1)}, bf16[128,768]{1,0:T(8,128)(2,1)S(1)}, u32[]{:S(2)}, u32[]{:S(2)}) collective-permute-start(bf16[128,768]{1,0:T(8,128)(2,1)S(1)} %get-tuple-element.55), channel_id=1, source_target_pairs={{0,2},{1,3},{2,0},{3,1},{4,6},{5,7},{6,4},{7,5},{8,10},{9,11},{10,... | collective-permute-start | bytes 589832 | tf_op jit(solution)/shard_map/ppermute | solution.py:468
  14.9 17.9 %collective-permute-start.6 = (bf16[128,768]{1,0:T(8,128)(2,1)S(1)}, bf16[128,768]{1,0:T(8,128)(2,1)S(1)}, u32[]{:S(2)}, u32[]{:S(2)}) collective-permute-start(bf16[128,768]{1,0:T(8,128)(2,1)S(1)} %get-tuple-element.56), channel_id=1, source_target_pairs={{0,3},{1,0},{2,1},{3,2},{4,7},{5,4},{6,5},{7,6},{8,11},{9,8},{10,9... | collective-permute-start | bytes 589832 | tf_op jit(solution)/shard_map/ppermute | solution.py:468
  22.6 17.8 %collective-permute-start.2 = (bf16[192,640]{1,0:T(8,128)(2,1)S(1)}, bf16[192,640]{1,0:T(8,128)(2,1)S(1)}, u32[]{:S(2)}, u32[]{:S(2)}) collective-permute-start(bf16[192,640]{1,0:T(8,128)(2,1)S(1)} %get-tuple-element.52), channel_id=1, source_target_pairs={{0,4},{4,8},{8,12},{12,16},{16,20},{20,24},{24,28},{28,0},{1,5},{5... | collective-permute-start | bytes 737288 | tf_op jit(solution)/shard_map/ppermute | solution.py:468
  24.3 16.1 %collective-permute-start.3 = (bf16[192,640]{1,0:T(8,128)(2,1)S(1)}, bf16[192,640]{1,0:T(8,128)(2,1)S(1)}, u32[]{:S(2)}, u32[]{:S(2)}) collective-permute-start(bf16[192,640]{1,0:T(8,128)(2,1)S(1)} %get-tuple-element.53), channel_id=1, source_target_pairs={{0,28},{4,0},{8,4},{12,8},{16,12},{20,16},{24,20},{28,24},{1,29},{... | collective-permute-start | bytes 737288 | tf_op jit(solution)/shard_map/ppermute | solution.py:468
  44.8 12.0 %collective-permute-start.7 = (bf16[128,256]{1,0:T(8,128)(2,1)S(1)}, bf16[128,256]{1,0:T(8,128)(2,1)S(1)}, u32[]{:S(2)}, u32[]{:S(2)}) collective-permute-start(bf16[128,256]{1,0:T(8,128)(2,1)S(1)} %get-tuple-element.63), channel_id=1, source_target_pairs={{0,1},{1,2},{2,3},{3,0},{4,5},{5,6},{6,7},{7,4},{8,9},{9,10},{10,1... | collective-permute-start | bytes 196616 | tf_op jit(solution)/shard_map/ppermute | solution.py:468
  45.5 11.3 %collective-permute-start.8 = (bf16[128,256]{1,0:T(8,128)(2,1)S(1)}, bf16[128,256]{1,0:T(8,128)(2,1)S(1)}, u32[]{:S(2)}, u32[]{:S(2)}) collective-permute-start(bf16[128,256]{1,0:T(8,128)(2,1)S(1)} %get-tuple-element.64), channel_id=1, source_target_pairs={{0,2},{1,3},{2,0},{3,1},{4,6},{5,7},{6,4},{7,5},{8,10},{9,11},{10,... | collective-permute-start | bytes 196616 | tf_op jit(solution)/shard_map/ppermute | solution.py:468
  50.2 6.5 %copy-start = (bf16[128,1,1,256]{3,0,2,1:T(8,128)(2,1)S(1)}, bf16[128,1,1,256]{3,0,2,1:T(8,128)(2,1)}, u32[]{:S(2)}) copy-start(bf16[128,1,1,256]{3,0,2,1:T(8,128)(2,1)} %param.25) | copy-start | bytes 196612
  50.3 6.5 %collective-permute-start.9 = (bf16[128,256]{1,0:T(8,128)(2,1)S(1)}, bf16[128,256]{1,0:T(8,128)(2,1)S(1)}, u32[]{:S(2)}, u32[]{:S(2)}) collective-permute-start(bf16[128,256]{1,0:T(8,128)(2,1)S(1)} %get-tuple-element.65), channel_id=1, source_target_pairs={{0,3},{1,0},{2,1},{3,2},{4,7},{5,4},{6,5},{7,6},{8,11},{9,8},{10,9... | collective-permute-start | bytes 196616 | tf_op jit(solution)/shard_map/ppermute | solution.py:468
